TPU v7x, 32 devices: a whole 2x2x4 slice. The times are simulated.
32 devices in a mesh: grp: 4 (over y, core), sub: 8 (over z, x).
Axes of the slice: x: 2, y: 2, z: 4, core: 2. Of those that a mesh axis runs over, the one named last changes fastest.
Arguments:
- fields: float32 [4, 35, 8192], P(None, None, ('grp', 'sub')), may hold values from -6 to 6
- section_store: float32 [4, 35, 8192], P(None, None, ('grp', 'sub')), may hold values from -6 to 6
- metric_terms: float32 [9, 8192], P(None, ('grp', 'sub')), may hold values from -6 to 6
- normals: float32 [4, 3, 8192], P(None, None, ('grp', 'sub')), may hold values from -3 to 3
- face_scale: float32 [4, 8192], P(None, ('grp', 'sub')), may hold values from 1 to 4
- damping: float32 [8192], P(('grp', 'sub')), may hold values from 1 to 10
- absorb_mask: int32 [8192], P(('grp', 'sub')), may hold values from 0 to 1
- refine_level: int32 [8192], P(('grp', 'sub')), may hold values from 0 to 2
- face_source: int32 [4, 8192], P(None, ('grp', 'sub')), may hold values from -1 to 1343, as said below
- orientation: int32 [4, 8192], P(None, ('grp', 'sub')), may hold values from 0 to 5, as said below
- derivative: float32 [3, 35, 35], replicated, may hold values from -1 to 1
- lift_matrix: float32 [35, 60], replicated, may hold values from -0.75 to 0.75
Outputs:
- fields_next: float32 [4, 35, 8192], P(None, None, ('grp', 'sub'))
- store_next: float32 [4, 35, 8192], P(None, None, ('grp', 'sub'))
- absorbed_energy: float32 [], replicated
Inputs may be any that keep to these rules, and one draw needn't show every extreme that they name: `face_source`: A device uses the slots of a block from rank 0 on without gaps; it never uses block s (its own sub index), nor block 8 at the first grp index or block 9 at the last. For a sub peer b with |b - s| <= 4 at most 32 ranks are used, for other peers at most 8, and across grp at most 32; in every draw some near pair uses all 32, some farther pair all 8, and some pair across grp all 32. Local neighbours lie on the same device. `orientation`: paired faces have inverse orientations: 1 and 2 swap, 0, 3, 4 and 5 stay.
All inputs are finite; a program needn't handle non-finite values.
Results may differ from a plain program's by a relative error of at most 0.0003.
Values sent between devices are 32-bit elements; how exact they have to be, the bound alone decides.
No kernel may reach another device: no remote copies, remote signals or barrier semaphores. Data moves between devices by JAX's collectives and lax.ppermute only.
A program may use at most 64 MiB of HBM per device.

v0:
```python
import jax
import jax.numpy as jnp
import numpy as np
from jax import lax
from jax.sharding import PartitionSpec as P

VOLUME_NODES = 35
FACE_NODES = 15


RUNGE_CARRY = -567301805773.0 / 1357537059087.0
RUNGE_ADVANCE = 5161836677717.0 / 13612068292357.0
TIME_STEP = 0.02


def passed_along(value, axis, steps):
    count = lax.axis_size(axis)
    first, last = (max(0, -steps), min(count, count - steps))
    return lax.ppermute(value, axis, [(source, source + steps) for source in range(first, last)])


def node_tables():
    volume_list = [
        (first_part, second_part, third_part, 4 - first_part - second_part - third_part)
        for first_part in range(5)
        for second_part in range(5 - first_part)
        for third_part in range(5 - first_part - second_part)
    ]
    triples = [
        (first_part, second_part, 4 - first_part - second_part)
        for first_part in range(5)
        for second_part in range(5 - first_part)
    ]
    face_index = np.zeros((4, 15), np.int32)
    for facet in range(4):
        others = [corner for corner in range(4) if corner != facet]
        for node_pos in range(15):
            corners = [0, 0, 0, 0]
            for place_pos in range(3):
                corners[others[place_pos]] = triples[node_pos][place_pos]
            face_index[facet, node_pos] = volume_list.index(tuple(corners))
    vertex_orders = [(0, 1, 2), (1, 2, 0), (2, 0, 1), (0, 2, 1), (2, 1, 0), (1, 0, 2)]
    turn_index = np.zeros((6, 15), np.int32)
    for option in range(6):
        vertex_order = vertex_orders[option]
        for node_pos in range(15):
            triple = triples[node_pos]
            turned = (triple[vertex_order[0]], triple[vertex_order[1]], triple[vertex_order[2]])
            turn_index[option, node_pos] = triples.index(turned)
    return (face_index, turn_index)


def turn_matrices():
    face_index, turn_index = node_tables()
    table = np.zeros((6, 15, 15), np.float32)
    for option in range(6):
        for node_pos in range(15):
            table[option, node_pos, turn_index[option, node_pos]] = 1.0
    return jnp.asarray(table, jnp.float32)


def pick_matrix():
    face_index, turn_index = node_tables()
    table = np.zeros((60, 35), np.float32)
    for node_pos in range(15):
        for facet in range(4):
            table[node_pos * 4 + facet, face_index[facet, node_pos]] = 1.0
    return jnp.asarray(table, jnp.float32)


def advance(
    fields,
    section_store,
    metric_terms,
    normals,
    face_scale,
    damping,
    absorb_mask,
    refine_level,
    face_codes,
    orient_flat,
    inner_cols,
    outer_cols,
    derivative,
    lift_matrix,
):
    elements_here = fields.shape[2]
    total_faces = 4 * elements_here
    turning = turn_matrices()
    inside = inner_cols.reshape(4, FACE_NODES, total_faces)
    gathered = outer_cols.reshape(4, FACE_NODES, total_faces)
    outside = gathered
    for option in range(1, 6):
        turned = jnp.einsum(
            "jk,ckx->cjx", turning[option], gathered, precision=lax.Precision.HIGHEST
        )
        outside = jnp.where(orient_flat[None, None, :] == option, turned, outside)
    normal_flat = jnp.transpose(normals, (1, 0, 2)).reshape(3, total_faces)
    on_wall = (face_codes < 0)[None, :]
    press_in = inside[0]
    veloc_in = inside[1:]
    normal_in = jnp.sum(normal_flat[:, None, :] * veloc_in, 0)
    press_out = jnp.where(on_wall, press_in, outside[0])
    veloc_out = jnp.where(
        on_wall[None], veloc_in - 2.0 * normal_flat[:, None, :] * normal_in[None], outside[1:]
    )
    press_jump = press_in - press_out
    normal_jump = jnp.sum(normal_flat[:, None, :] * (veloc_in - veloc_out), 0)
    growth = jnp.exp2(refine_level.astype(jnp.float32))
    weight_face = (face_scale * growth[None, :]).reshape(total_faces)
    flux_press = 0.5 * weight_face[None, :] * (normal_jump - press_jump)
    flux_veloc = (
        0.5
        * weight_face[None, None, :]
        * normal_flat[:, None, :]
        * (press_jump - normal_jump)[None]
    )
    flux_all = jnp.concatenate([flux_press[None], flux_veloc], 0).reshape(
        4, FACE_NODES, 4, elements_here
    )
    lifted = jnp.einsum(
        "nfj,cjfe->cne",
        lift_matrix.reshape(VOLUME_NODES, 4, FACE_NODES),
        flux_all,
        precision=lax.Precision.HIGHEST,
    )
    slopes = jnp.einsum("dnm,cme->dcne", derivative, fields, precision=lax.Precision.HIGHEST)
    metric = metric_terms.reshape(3, 3, elements_here) * growth[None, None, :]
    physical = jnp.einsum("ide,dcne->icne", metric, slopes, precision=lax.Precision.HIGHEST)
    absorb = damping * absorb_mask.astype(jnp.float32)
    diverge = physical[0, 1] + physical[1, 2] + physical[2, 3]
    volume = jnp.concatenate([-diverge[None], -physical[:, 0]], 0)
    change = volume + lifted - absorb[None, None, :] * fields
    store_next = RUNGE_CARRY * section_store + TIME_STEP * change
    fields_next = fields + RUNGE_ADVANCE * store_next
    energy = jnp.sum(absorb * jnp.sum(fields_next * fields_next, (0, 1)))
    return (fields_next, store_next, energy)


def local(
    fields,
    section_store,
    metric_terms,
    normals,
    face_scale,
    damping,
    absorb_mask,
    refine_level,
    face_source,
    orientation,
    derivative,
    lift_matrix,
):
    elements_here = fields.shape[2]
    total_faces = 4 * elements_here
    slot_width = elements_here // 8
    peer_count = lax.axis_size("sub")
    block_total = peer_count + 2
    row_count = 4 * FACE_NODES
    picker = pick_matrix()
    traces = jnp.einsum("kn,cne->cke", picker, fields, precision=lax.Precision.HIGHEST)
    inner_cols = traces.reshape(row_count, total_faces)
    face_codes = face_source.reshape(total_faces)
    orient_flat = orientation.reshape(total_faces)
    remote = face_codes >= total_faces
    slot_index = jnp.where(remote, face_codes - total_faces, 0)
    block_index = jnp.where(remote, slot_index // slot_width, block_total)
    within = slot_index % slot_width
    outbox = (
        jnp.zeros((block_total, row_count, slot_width), jnp.float32)
        .at[block_index, :, within]
        .set(inner_cols.T, mode="drop")
    )
    arrived = lax.all_to_all(outbox[:peer_count], "sub", split_axis=0, concat_axis=0, tiled=True)
    from_below = passed_along(outbox[peer_count + 1], "grp", 1)
    from_above = passed_along(outbox[peer_count], "grp", -1)
    received = jnp.concatenate([arrived, from_below[None], from_above[None]], 0)
    local_side = (face_codes >= 0) & (face_codes < total_faces)
    own_pick = jnp.take(inner_cols, jnp.clip(face_codes, 0, total_faces - 1), axis=1)
    far_pick = received[jnp.minimum(block_index, block_total - 1), :, within].T
    outer_cols = jnp.where(local_side[None, :], own_pick, jnp.where(remote[None, :], far_pick, 0.0))
    fields_next, store_next, energy = advance(
        fields,
        section_store,
        metric_terms,
        normals,
        face_scale,
        damping,
        absorb_mask,
        refine_level,
        face_codes,
        orient_flat,
        inner_cols,
        outer_cols,
        derivative,
        lift_matrix,
    )
    summed = lax.psum(energy, ("grp", "sub"))
    divisor = elements_here * lax.axis_size("grp") * peer_count * VOLUME_NODES
    return (fields_next, store_next, summed / divisor)


def solution(mesh):
    placed = (
        P(None, None, ("grp", "sub")),
        P(None, None, ("grp", "sub")),
        P(None, ("grp", "sub")),
        P(None, None, ("grp", "sub")),
        P(None, ("grp", "sub")),
        P(("grp", "sub")),
        P(("grp", "sub")),
        P(("grp", "sub")),
        P(None, ("grp", "sub")),
        P(None, ("grp", "sub")),
        P(),
        P(),
    )
    return jax.shard_map(
        local,
        mesh=mesh,
        in_specs=placed,
        out_specs=(P(None, None, ("grp", "sub")), P(None, None, ("grp", "sub")), P()),
        check_vma=False,
    )
```

profile of v0, /device:TPU:0, one launch (start us, length us, event | category | flops | bytes accessed | tf_op | source)
XLA Modules:
  0.0 93.0 jit_solution(12577065569815034007)
XLA Ops:
  0.7 0.7 broadcast_compare_fusion.6
  1.4 0.7 clamp_bitcast_fusion.1
  2.2 0.7 multiply_reduce_fusion.2
  2.9 0.8 and_reduce_fusion
  3.7 1.3 %convolution_bitcast_fusion.6 = f32[4,60,256]{2,1,0:T(8,128)S(1)} fusion(f32[60,35,1]{0,1,2:T(8,128)} %constant.119, f32[4,35,256]{2,0,1:T(4,128)} %param.14), kind=kOutput, calls=%fused_computation.14 | convolution fusion | flops 25804800 | bytes 397520 | tf_op jit(solution)/shard_map/kn,cne->cke/dot_general | solution.py:161
  5.4 3.1 %scatter_custom_fusion = f32[320,60]{1,0:T(8,128)S(1)} fusion(s32[1024]{0:T(1024)S(1)} %broadcast_select_fusion, f32[1024,60]{1,0:T(8,128)S(1)} %copy.100, f32[]{:T(128)} %constant.36.clone.1), kind=kCustom, calls=%fused_computation.42 | custom fusion | bytes 76804
  8.5 0.6 slice_bitcast_fusion.1
  9.1 2.4 %collective-permute-start = (f32[60,32]{0,1:T(8,128)}, f32[60,32]{0,1:T(8,128)S(1)}, u32[]{:S(2)}, u32[]{:S(2)}) collective-permute-start(f32[60,32]{0,1:T(8,128)} %get-tuple-element.25), channel_id=1, source_target_pairs={{0,8},{8,16},{16,24},{1,9},{9,17},{17,25},{2,10},{10,18},{18,26},{... | collective-permute-start | bytes 23048 | tf_op jit(solution)/shard_map/ppermute | solution.py:19
  11.5 1.3 %collective-permute-start.1 = (f32[60,32]{0,1:T(8,128)S(1)}, f32[60,32]{0,1:T(8,128)S(1)}, u32[]{:S(2)}, u32[]{:S(2)}) collective-permute-start(f32[60,32]{0,1:T(8,128)S(1)} %get-tuple-element.26), channel_id=1, source_target_pairs={{8,0},{16,8},{24,16},{9,1},{17,9},{25,17},{10,2},{18,10},{26,18},{... | collective-permute-start | bytes 23048 | tf_op jit(solution)/shard_map/ppermute | solution.py:19
  12.8 0.8 reshape.426
  13.6 6.6 %all-to-all-start = ((f32[8,1,1920]{2,1,0:T(1,128)}), f32[8,1,1920]{2,1,0:T(1,128)S(1)}, u32[]{:S(2)}, u32[]{:S(2)}) async-start(f32[8,1,1920]{2,1,0:T(1,128)} %reshape.426), calls=%async_computation | async-start | bytes 122880 | tf_op jit(solution)/shard_map/all_to_all | solution.py:174
  20.3 0.5 convolution_bitcast_fusion
  20.9 1.4 %copy.96 = f32[3,4,35,256]{2,0,1,3:T(4,128)S(1)} copy(f32[3,4,35,256]{3,2,0,1:T(8,128)S(1)} %convolution_bitcast_fusion) | data formatting | bytes 860160 | tf_op jit(solution)/shard_map/dnm,cme->dcne/transpose | solution.py:127
  22.5 5.3 %fusion.5 = f32[256,4,35,3]{2,3,1,0:T(4,128)} fusion(f32[3,4,35,256]{2,0,1,3:T(4,128)S(1)} %copy.96, f32[3,3,256]{1,0,2:T(4,128)S(1)} %copy.95, f32[256]{0:T(256)S(1)} %multiply_exponential_fusion), kind=kOutput, calls=%fused_computation.16 | convolution fusion | flops 3873024 | bytes 870400 | tf_op jit(solution)/shard_map/ide,dcne->icne/dot_general | solution.py:129
  27.8 2.0 %copy.97 = f32[256,4,35,3]{0,3,2,1:T(4,128)S(1)} copy(f32[256,4,35,3]{2,3,1,0:T(4,128)} %fusion.5) | data formatting | bytes 860160 | tf_op jit(solution)/shard_map/ide,dcne->icne/dot_general | solution.py:129
  30.0 0.5 compare_and_fusion
  31.4 2.8 %gather_fusion = f32[1024,60]{1,0:T(8,128)S(1)} fusion(f32[60,1024]{0,1:T(8,128)S(1)} %copy.99, s32[1024]{0:T(1024)S(1)} %broadcast_clamp_fusion), kind=kCustom, calls=%fused_computation | custom fusion | bytes 495616 | tf_op jit(solution)/shard_map/jit(_take)/gather | solution.py:179
  34.2 0.5 broadcast.470
  34.7 0.8 reduce.5
  35.8 6.8 %gather_fusion.1 = f32[1024,60]{1,0:T(8,128)S(1)} fusion(f32[10,60,32]{1,2,0:T(8,128)S(1)} %pad_maximum_fusion, s32[1024]{0:T(1024)S(1)} %bitcast.111), kind=kCustom, calls=%fused_computation.1 | custom fusion | bytes 499712 | tf_op jit(solution)/shard_map/gather | solution.py:180
  42.6 0.8 select_bitcast_fusion
  46.2 0.9 multiply_reduce_fusion.1
  47.1 0.6 multiply_reduce_fusion.3
  47.7 43.4 %psum.7 = f32[]{:T(128)} all-reduce(f32[]{:T(128)} %multiply_reduce_fusion.3), channel_id=1, replica_groups=mesh['grp'=4,'sub'=8] {'grp','sub'}, use_global_device_ids=true, to_apply=%region_5.6 | all-reduce | flops 1 | bytes 8 | tf_op jit(solution)/shard_map/psum | solution.py:198
  (97 shorter events, 4.3 us)
Async XLA Ops:
  0.6 19.7 %copy-start = (f32[3,35,35]{2,1,0:T(8,128)S(1)}, f32[3,35,35]{2,1,0:T(8,128)}, u32[]{:S(2)}) copy-start(f32[3,35,35]{2,1,0:T(8,128)} %param.24) | copy-start | bytes 44104
  0.6 19.7 %copy-start.1 = (f32[4,35,256]{2,0,1:T(4,128)S(1)}, f32[4,35,256]{2,0,1:T(4,128)}, u32[]{:S(2)}) copy-start(f32[4,35,256]{2,0,1:T(4,128)} %param.14) | copy-start | bytes 430084
  0.7 19.6 %copy-start.16 = (s32[256]{0:T(256)S(1)}, s32[256]{0:T(256)}, u32[]{:S(2)}) copy-start(s32[256]{0:T(256)} %param.21) | copy-start | bytes 3076
  0.7 19.6 %copy-start.6 = (f32[4,256]{1,0:T(4,128)S(1)}, f32[4,256]{1,0:T(4,128)}, u32[]{:S(2)}) copy-start(f32[4,256]{1,0:T(4,128)} %param.18) | copy-start | bytes 12292
  5.4 16.9 %copy-start.5 = (f32[9,256]{1,0:T(8,128)S(1)}, f32[9,256]{1,0:T(8,128)}, u32[]{:S(2)}) copy-start(f32[9,256]{1,0:T(8,128)} %param.16) | copy-start | bytes 27652
  9.1 26.6 %collective-permute-start = (f32[60,32]{0,1:T(8,128)}, f32[60,32]{0,1:T(8,128)S(1)}, u32[]{:S(2)}, u32[]{:S(2)}) collective-permute-start(f32[60,32]{0,1:T(8,128)} %get-tuple-element.25), channel_id=1, source_target_pairs={{0,8},{8,16},{16,24},{1,9},{9,17},{17,25},{2,10},{10,18},{18,26},{... | collective-permute-start | bytes 23048 | tf_op jit(solution)/shard_map/ppermute | solution.py:19
  11.5 24.2 %collective-permute-start.1 = (f32[60,32]{0,1:T(8,128)S(1)}, f32[60,32]{0,1:T(8,128)S(1)}, u32[]{:S(2)}, u32[]{:S(2)}) collective-permute-start(f32[60,32]{0,1:T(8,128)S(1)} %get-tuple-element.26), channel_id=1, source_target_pairs={{8,0},{16,8},{24,16},{9,1},{17,9},{25,17},{10,2},{18,10},{26,18},{... | collective-permute-start | bytes 23048 | tf_op jit(solution)/shard_map/ppermute | solution.py:19
  13.6 20.6 %all-to-all-start = ((f32[8,1,1920]{2,1,0:T(1,128)}), f32[8,1,1920]{2,1,0:T(1,128)S(1)}, u32[]{:S(2)}, u32[]{:S(2)}) async-start(f32[8,1,1920]{2,1,0:T(1,128)} %reshape.426), calls=%async_computation | async-start | bytes 122880 | tf_op jit(solution)/shard_map/all_to_all | solution.py:174
  27.8 2.8 %copy-start.12 = (s32[4,256]{1,0:T(4,128)S(1)}, s32[4,256]{1,0:T(4,128)}, u32[]{:S(2)}) copy-start(s32[4,256]{1,0:T(4,128)} %param.23) | copy-start | bytes 12292
  27.8 2.8 %copy-start.3 = (f32[4,3,256]{2,0,1:T(4,128)S(1)}, f32[4,3,256]{2,0,1:T(4,128)}, u32[]{:S(2)}) copy-start(f32[4,3,256]{2,0,1:T(4,128)} %param.17) | copy-start | bytes 36868
  27.8 3.0 %copy-start.14 = (f32[256]{0:T(256)S(1)}, f32[256]{0:T(256)}, u32[]{:S(2)}) copy-start(f32[256]{0:T(256)} %param.19) | copy-start | bytes 3076
  27.8 3.0 %copy-start.15 = (s32[256]{0:T(256)S(1)}, s32[256]{0:T(256)}, u32[]{:S(2)}) copy-start(s32[256]{0:T(256)} %param.20) | copy-start | bytes 3076
  29.8 1.4 %copy-start.4 = (f32[35,60]{1,0:T(8,128)S(1)}, f32[35,60]{1,0:T(8,128)}, u32[]{:S(2)}) copy-start(f32[35,60]{1,0:T(8,128)} %param.25) | copy-start | bytes 25204
  35.7 6.8 %copy-start.13 = (pred[1024]{0:T(1024)(128)(4,1)S(1)}, pred[1024]{0:T(1024)(128)(4,1)}, u32[]{:S(2)}) copy-start(pred[1024]{0:T(1024)(128)(4,1)} %compare_and_fusion) | copy-start | bytes 3076
  42.6 1.2 %copy-start.11 = (f32[15,15,1]{1,0,2:T(8,128)S(1)}, f32[15,15,1]{1,0,2:T(8,128)}, u32[]{:S(2)}) copy-start(f32[15,15,1]{1,0,2:T(8,128)} %constant.123) | copy-start | bytes 2704
  42.6 1.5 %copy-start.10 = (f32[15,15,1]{1,0,2:T(8,128)S(1)}, f32[15,15,1]{1,0,2:T(8,128)}, u32[]{:S(2)}) copy-start(f32[15,15,1]{1,0,2:T(8,128)} %constant.122) | copy-start | bytes 2704
  42.6 1.9 %copy-start.9 = (f32[15,15,1]{1,0,2:T(8,128)S(1)}, f32[15,15,1]{1,0,2:T(8,128)}, u32[]{:S(2)}) copy-start(f32[15,15,1]{1,0,2:T(8,128)} %constant.120) | copy-start | bytes 2704
  42.6 2.2 %copy-start.8 = (f32[15,15,1]{1,0,2:T(8,128)S(1)}, f32[15,15,1]{1,0,2:T(8,128)}, u32[]{:S(2)}) copy-start(f32[15,15,1]{1,0,2:T(8,128)} %constant.124) | copy-start | bytes 2704
  43.5 1.8 %copy-start.7 = (f32[15,15,1]{1,0,2:T(8,128)S(1)}, f32[15,15,1]{1,0,2:T(8,128)}, u32[]{:S(2)}) copy-start(f32[15,15,1]{1,0,2:T(8,128)} %constant.121) | copy-start | bytes 2704
  44.8 1.4 %copy-start.2 = (f32[4,35,256]{2,0,1:T(4,128)S(1)}, f32[4,35,256]{2,0,1:T(4,128)}, u32[]{:S(2)}) copy-start(f32[4,35,256]{2,0,1:T(4,128)} %param.15) | copy-start | bytes 430084
where the time goes:
time: 93.5 us; the launch traced here: 93 us
  blocking collectives  43.4 us (46%)
  local copies, waits for them, and re-layouts  19.8 us (21%)
  starting transfers between devices  10.3 us (11%)
  matrix products  9.29 us (10%)
  other arithmetic  7 us (7%)
  between operations  3.13 us (3%)
    psum x1, blocking collectives, local(): summed = lax.psum(energy, ('grp', 'sub'))  43.4 us
    gather x1, local copies, waits for them, and re-layouts, local(): far_pick = received[jnp.minimum(block_index, block_total - 1), :, within].T  6.79 us
    all_to_all x1, starting transfers between devices, local(): lax.all_to_all(outbox[:peer_count], 'sub', split_axis=0, concat_axis=0, t...  6.62 us
    dot_general x1, matrix products, advance(): jnp.einsum('ide,dcne->icne', metric, slopes, precision=lax.Precision.HIGH...  5.26 us
    unnamed x45, local copies, waits for them, and re-layouts  4.35 us
    ppermute x2, starting transfers between devices, passed_along(): lax.ppermute(value, axis, [(source, source + steps) for source in range(f...  3.68 us
    gather x1, local copies, waits for them, and re-layouts, local(): jnp.take(inner_cols, jnp.clip(face_codes, 0, total_faces - 1), axis=1)  2.8 us
    unnamed x5, other arithmetic  2.19 us
  transfers between devices with their start and end apart: 3, of which 0 were waited for; matrix products, arithmetic and copies ran while one was open for 17% of the time, Pallas kernels for 0%

commit v1 on v0

v1 whole, which is shorter than its diff:
```python
import jax
import jax.numpy as jnp
import numpy as np
from jax import lax
from jax.experimental import pallas as pl
from jax.experimental.pallas import tpu as pltpu
from jax.sharding import PartitionSpec as P

VOLUME_NODES = 35
FACE_NODES = 15
ROWS = 16

RUNGE_CARRY = -567301805773.0 / 1357537059087.0
RUNGE_ADVANCE = 5161836677717.0 / 13612068292357.0
TIME_STEP = 0.02
INVERSE_TURN = (0, 2, 1, 3, 4, 5)


def node_tables():
    volume_list = [
        (a, b, c, 4 - a - b - c)
        for a in range(5)
        for b in range(5 - a)
        for c in range(5 - a - b)
    ]
    triples = [(a, b, 4 - a - b) for a in range(5) for b in range(5 - a)]
    face_index = np.zeros((4, 15), np.int32)
    for facet in range(4):
        others = [corner for corner in range(4) if corner != facet]
        for node_pos in range(15):
            corners = [0, 0, 0, 0]
            for place_pos in range(3):
                corners[others[place_pos]] = triples[node_pos][place_pos]
            face_index[facet, node_pos] = volume_list.index(tuple(corners))
    vertex_orders = [(0, 1, 2), (1, 2, 0), (2, 0, 1), (0, 2, 1), (2, 1, 0), (1, 0, 2)]
    turn_index = np.zeros((6, 15), np.int32)
    for option in range(6):
        order = vertex_orders[option]
        for node_pos in range(15):
            triple = triples[node_pos]
            turned = (triple[order[0]], triple[order[1]], triple[order[2]])
            turn_index[option, node_pos] = triples.index(turned)
    return face_index, turn_index


FACE_INDEX, TURN_INDEX = node_tables()


def split_three(value):
    high = value.astype(jnp.bfloat16)
    rest = value - high.astype(jnp.float32)
    middle = rest.astype(jnp.bfloat16)
    low = (rest - middle.astype(jnp.float32)).astype(jnp.bfloat16)
    return high, middle, low


def turned_traces(fields_ref, orient_ref, turned_ref, elements_here):
    for facet in range(4):
        for start in range(0, elements_here, 128):
            lanes = slice(start, start + 128)
            tile = (facet * elements_here + start) // 128
            own_turn = jnp.broadcast_to(orient_ref[facet : facet + 1, lanes], (4, 128))
            is_turn = [own_turn == option for option in range(6)]
            nodes = [fields_ref[int(FACE_INDEX[facet, j]), :, lanes] for j in range(FACE_NODES)]
            for j in range(FACE_NODES):
                by_source = {}
                for option in range(6):
                    source = int(TURN_INDEX[INVERSE_TURN[option], j])
                    by_source.setdefault(source, []).append(option)
                items = list(by_source.items())
                value = nodes[items[0][0]]
                for source, options in items[1:]:
                    mask = is_turn[options[0]]
                    for option in options[1:]:
                        mask = mask | is_turn[option]
                    value = jnp.where(mask, nodes[source], value)
                turned_ref[tile, pl.ds(j, 4, stride=ROWS), :] = value
            turned_ref[tile, pl.ds(15, 4, stride=ROWS), :] = jnp.zeros((4, 128), jnp.float32)


def side_by_side(tiles_ref):
    return jnp.concatenate([tiles_ref[tile] for tile in range(tiles_ref.shape[0])], 1)


def code_row(code_ref, facet):
    return code_ref[facet : facet + 1, :]


def slot_hits(code_ref, slots, total_faces):
    parts = []
    for facet in range(4):
        codes = code_row(code_ref, facet) - total_faces
        rows = lax.broadcasted_iota(jnp.int32, (slots, codes.shape[1]), 0)
        parts.append(jnp.where(rows == codes, 1.0, 0.0).astype(jnp.bfloat16))
    return jnp.concatenate(parts, 1)


def pack_kernel(peers, fields_ref, code_ref, orient_ref, near_ref, up_ref, down_ref, turned_ref):
    elements_here = fields_ref.shape[2]
    total_faces = 4 * elements_here
    width = elements_here // 8
    blocks = peers + 2
    turned_traces(fields_ref, orient_ref, turned_ref, elements_here)
    parts = jnp.concatenate(split_three(side_by_side(turned_ref)), 0)
    hits = slot_hits(code_ref, blocks * width, total_faces)
    packed = lax.dot_general(
        parts, hits, (((1,), (1,)), ((), ())), preferred_element_type=jnp.float32
    )
    rows = 4 * ROWS
    packed = packed[:rows] + (packed[rows : 2 * rows] + packed[2 * rows :])
    for block in range(blocks):
        columns = slice(block * width, (block + 1) * width)
        value = jnp.concatenate(
            [packed[c * ROWS : (c + 1) * ROWS, columns] for c in range(4)], 1
        )
        if block < peers:
            near_ref[block] = value
        elif block == peers:
            down_ref[...] = value
        else:
            up_ref[...] = value


def inner_kernel(
    fields_ref,
    store_ref,
    metric_ref,
    normal_ref,
    scale_ref,
    damping_ref,
    mask_ref,
    level_ref,
    code_ref,
    orient_ref,
    derivative_ref,
    lift_ref,
    base_ref,
    plain_ref,
    flux_ref,
    weight_ref,
    absorb_ref,
    lift_out_ref,
    turned_ref,
    trace_ref,
):
    elements_here = fields_ref.shape[2]
    total_faces = 4 * elements_here
    growth = jnp.exp2(level_ref[...].astype(jnp.float32))
    absorb = damping_ref[...] * mask_ref[...].astype(jnp.float32)
    absorb_ref[...] = absorb
    weight_ref[...] = 0.5 * (scale_ref[...] * growth)
    plain = [fields_ref[:, c, :] for c in range(4)]
    for c in range(4):
        plain_ref[c] = plain[c]
    joined = jnp.concatenate(plain, 1)
    slopes = [
        jnp.dot(
            derivative_ref[y],
            joined,
            precision=lax.Precision.HIGHEST,
            preferred_element_type=jnp.float32,
        )
        for y in range(3)
    ]

    def slope(y, c):
        return slopes[y][:, c * elements_here : (c + 1) * elements_here]

    metric = metric_ref[...] * growth

    def physical(x, c):
        total = metric[3 * x : 3 * x + 1] * slope(0, c)
        for y in (1, 2):
            total = total + metric[3 * x + y : 3 * x + y + 1] * slope(y, c)
        return total

    for c in range(4):
        if c == 0:
            volume = physical(0, 1) + physical(1, 2) + physical(2, 3)
        else:
            volume = physical(c - 1, 0)
        change = -volume - absorb * plain[c]
        base_ref[c] = RUNGE_CARRY * store_ref[:, c, :] + TIME_STEP * change
    for facet in range(4):
        for tile in range(elements_here // 128):
            for j in range(ROWS):
                if j < FACE_NODES:
                    node = int(FACE_INDEX[facet, j])
                    value = fields_ref[node, :, tile * 128 : tile * 128 + 128]
                else:
                    value = jnp.zeros((4, 128), jnp.float32)
                trace_ref[tile, pl.ds(facet * ROWS + j, 4, stride=4 * ROWS), :] = value
    traces = side_by_side(trace_ref)
    turned_traces(fields_ref, orient_ref, turned_ref, elements_here)
    parts = jnp.concatenate(split_three(side_by_side(turned_ref)), 0)
    rows = 4 * ROWS
    for facet in range(4):
        codes = code_row(code_ref, facet)
        hits = jnp.where(
            lax.broadcasted_iota(jnp.int32, (total_faces, elements_here), 0) == codes, 1.0, 0.0
        ).astype(jnp.bfloat16)
        found = jnp.dot(parts, hits, preferred_element_type=jnp.float32)
        found = found[:rows] + (found[rows : 2 * rows] + found[2 * rows :])
        inside = [
            traces[c * rows + facet * ROWS : c * rows + facet * ROWS + ROWS] for c in range(4)
        ]
        outside = [found[c * ROWS : (c + 1) * ROWS] for c in range(4)]
        normal = [normal_ref[x, facet : facet + 1, :] for x in range(3)]
        wall = codes < 0
        normal_in = normal[0] * inside[1] + normal[1] * inside[2] + normal[2] * inside[3]
        press_jump = jnp.where(wall, 0.0, inside[0] - outside[0])
        normal_jump = jnp.zeros_like(press_jump)
        for x in range(3):
            step = jnp.where(
                wall, 2.0 * normal[x] * normal_in, inside[1 + x] - outside[1 + x]
            )
            normal_jump = normal_jump + normal[x] * step
        weight = 0.5 * (scale_ref[facet : facet + 1, :] * growth)
        flux_ref[facet * ROWS : (facet + 1) * ROWS, :] = weight * (normal_jump - press_jump)
    wide = lax.broadcasted_iota(jnp.int32, (4 * FACE_NODES, rows), 1)
    tall = lax.broadcasted_iota(jnp.int32, (4 * FACE_NODES, rows), 0)
    facet_of = wide // ROWS
    place = jnp.where(
        (tall == wide - facet_of) & (wide - facet_of * ROWS < FACE_NODES), 1.0, 0.0
    )
    spread = jnp.dot(
        lift_ref[...],
        place,
        precision=lax.Precision.HIGHEST,
        preferred_element_type=jnp.float32,
    )
    high, middle, low = split_three(spread)
    lift_out_ref[...] = jnp.concatenate([high, high, middle, middle], 1)


def outer_kernel(
    peers,
    near_ref,
    below_ref,
    above_ref,
    code_ref,
    normal_ref,
    weight_ref,
    flux_ref,
    lift_ref,
    base_ref,
    plain_ref,
    absorb_ref,
    fields_ref,
    store_ref,
    energy_ref,
):
    elements_here = plain_ref.shape[2]
    total_faces = 4 * elements_here
    width = elements_here // 8
    blocks = peers + 2
    rows = 4 * ROWS
    boxes = [near_ref[block] for block in range(peers)] + [below_ref[...], above_ref[...]]
    received = jnp.concatenate(
        [
            jnp.concatenate([box[:, c * width : (c + 1) * width] for box in boxes], 1)
            for c in range(4)
        ],
        0,
    )
    parts = jnp.concatenate(split_three(received), 0)
    hits = slot_hits(code_ref, blocks * width, total_faces)
    found = jnp.dot(parts, hits, preferred_element_type=jnp.float32)
    found = found[:rows] + (found[rows : 2 * rows] + found[2 * rows :])
    pieces = []
    for facet in range(4):
        columns = slice(facet * elements_here, (facet + 1) * elements_here)
        outside = [found[c * ROWS : (c + 1) * ROWS, columns] for c in range(4)]
        normal = [normal_ref[x, facet : facet + 1, :] for x in range(3)]
        across = normal[0] * outside[1] + normal[1] * outside[2] + normal[2] * outside[3]
        weight = weight_ref[facet : facet + 1, :]
        press = flux_ref[facet * ROWS : (facet + 1) * ROWS, :] + weight * (outside[0] - across)
        pieces.append([press] + [-normal[x] * press for x in range(3)])
    flux = jnp.concatenate(
        [jnp.concatenate([pieces[facet][c] for facet in range(4)], 0) for c in range(4)], 1
    )
    high = flux.astype(jnp.bfloat16)
    middle = (flux - high.astype(jnp.float32)).astype(jnp.bfloat16)
    lifted = jnp.dot(
        lift_ref[...],
        jnp.concatenate([high, middle, high, middle], 0),
        preferred_element_type=jnp.float32,
    )
    square = jnp.zeros((VOLUME_NODES, elements_here), jnp.float32)
    for c in range(4):
        columns = slice(c * elements_here, (c + 1) * elements_here)
        store_next = base_ref[c] + TIME_STEP * lifted[:, columns]
        fields_next = plain_ref[c] + RUNGE_ADVANCE * store_next
        store_ref[:, c, :] = store_next
        fields_ref[:, c, :] = fields_next
        square = square + fields_next * fields_next
    energy = jnp.sum(square, 0, keepdims=True) * absorb_ref[...]
    total = energy[:, :128]
    for start in range(128, elements_here, 128):
        total = total + energy[:, start : start + 128]
    energy_ref[...] = jnp.broadcast_to(total[None], energy_ref.shape)


def local(
    fields,
    section_store,
    metric_terms,
    normals,
    face_scale,
    damping,
    absorb_mask,
    refine_level,
    face_source,
    orientation,
    derivative,
    lift_matrix,
):
    elements_here = fields.shape[2]
    total_faces = 4 * elements_here
    peers = lax.axis_size("sub")
    slabs = lax.axis_size("grp")
    devices = peers * slabs
    f32 = jnp.float32
    fields_t = jnp.transpose(fields, (1, 0, 2))
    store_t = jnp.transpose(section_store, (1, 0, 2))
    normals_t = jnp.transpose(normals, (1, 0, 2))
    row = (1, elements_here)
    near, up, down = pl.pallas_call(
        lambda *refs: pack_kernel(peers, *refs),
        out_shape=(
            jax.ShapeDtypeStruct((peers, ROWS, 128), f32),
            jax.ShapeDtypeStruct((ROWS, 128), f32),
            jax.ShapeDtypeStruct((ROWS, 128), f32),
        ),
        scratch_shapes=[pltpu.VMEM((total_faces // 128, 4 * ROWS, 128), f32)],
        name="pack",
    )(fields_t, face_source, orientation)
    arrived = lax.all_to_all(near, "sub", split_axis=0, concat_axis=0, tiled=True)
    from_below = lax.ppermute(up, "grp", [(g, g + 1) for g in range(slabs - 1)])
    from_above = lax.ppermute(down, "grp", [(g + 1, g) for g in range(slabs - 1)])
    base, plain, flux, weight, absorb, lift_parts = pl.pallas_call(
        inner_kernel,
        out_shape=(
            jax.ShapeDtypeStruct((4, VOLUME_NODES, elements_here), f32),
            jax.ShapeDtypeStruct((4, VOLUME_NODES, elements_here), f32),
            jax.ShapeDtypeStruct((4 * ROWS, elements_here), f32),
            jax.ShapeDtypeStruct((4, elements_here), f32),
            jax.ShapeDtypeStruct(row, f32),
            jax.ShapeDtypeStruct((VOLUME_NODES, 16 * ROWS), jnp.bfloat16),
        ),
        scratch_shapes=[
            pltpu.VMEM((total_faces // 128, 4 * ROWS, 128), f32),
            pltpu.VMEM((elements_here // 128, 16 * ROWS, 128), f32),
        ],
        name="inner",
    )(
        fields_t,
        store_t,
        metric_terms,
        normals_t,
        face_scale,
        damping.reshape(row),
        absorb_mask.reshape(row),
        refine_level.reshape(row),
        face_source,
        orientation,
        derivative,
        lift_matrix,
    )
    fields_next, store_next, energy = pl.pallas_call(
        lambda *refs: outer_kernel(peers, *refs),
        out_shape=(
            jax.ShapeDtypeStruct((VOLUME_NODES, 4, elements_here), f32),
            jax.ShapeDtypeStruct((VOLUME_NODES, 4, elements_here), f32),
            jax.ShapeDtypeStruct((devices, 1, 128), f32),
        ),
        name="outer",
    )(
        arrived,
        from_below,
        from_above,
        face_source,
        normals_t,
        weight,
        flux,
        lift_parts,
        base,
        plain,
        absorb,
    )
    shares = lax.all_to_all(energy, ("grp", "sub"), split_axis=0, concat_axis=0, tiled=True)
    divisor = elements_here * devices * VOLUME_NODES
    return (
        jnp.transpose(fields_next, (1, 0, 2)),
        jnp.transpose(store_next, (1, 0, 2)),
        jnp.sum(shares) / divisor,
    )


def solution(mesh):
    placed = (
        P(None, None, ("grp", "sub")),
        P(None, None, ("grp", "sub")),
        P(None, ("grp", "sub")),
        P(None, None, ("grp", "sub")),
        P(None, ("grp", "sub")),
        P(("grp", "sub")),
        P(("grp", "sub")),
        P(("grp", "sub")),
        P(None, ("grp", "sub")),
        P(None, ("grp", "sub")),
        P(),
        P(),
    )
    return jax.shard_map(
        local,
        mesh=mesh,
        in_specs=placed,
        out_specs=(P(None, None, ("grp", "sub")), P(None, None, ("grp", "sub")), P()),
        check_vma=False,
    )
```

time: 93.5 us -> 38.2 us (0.41)
  blocking collectives: 43.4 us -> 15.1 us
  local copies, waits for them, and re-layouts: 19.8 us -> 0.62 us
  matrix products: 9.29 us -> 0 us
  Pallas kernels: 0 us -> 7.96 us
  other arithmetic: 7 us -> 0.63 us
    psum x1 -> x0, blocking collectives: 43.4 us -> none  [local(): summed = lax.psum(energy, ('grp', 'sub'))]
    all_to_all x0 -> x1, blocking collectives: none -> 15.1 us  [local(): lax.all_to_all(energy, ('grp', 'sub'), split_axis=0, concat_axis=0, tiled...]
    gather x2 -> x0, local copies, waits for them, and re-layouts: 9.59 us -> none  [the longest x1 6.79 us: local(): far_pick = received[jnp.minimum(block_index, block_total - 1), :, within].T]
    dot_general x9 -> x0, matrix products: 9.29 us -> none  [the longest x1 5.26 us: advance(): jnp.einsum('ide,dcne->icne', metric, slopes, precision=lax.Precision.HIGH...]
    pallas_call x0 -> x3, Pallas kernels: none -> 7.96 us  [the longest x1 3.17 us: local(): pl.pallas_call(inner_kernel, out_shape=(jax.ShapeDtypeStruct((4, VOLUME_N...]
    unnamed x45 -> x10, local copies, waits for them, and re-layouts: 4.35 us -> 0.62 us
    unnamed x5 -> x0, other arithmetic: 2.19 us -> none
    dot_general x1 -> x0, local copies, waits for them, and re-layouts: 2.01 us -> none  [advance(): jnp.einsum('ide,dcne->icne', metric, slopes, precision=lax.Precision.HIGH...]
  transfers between devices with their start and end apart: 3 -> 3, of which waited for: 0 -> 2; matrix products, arithmetic and copies ran while one was open for 17% -> 0% of each run, Pallas kernels for 0% -> 8%
where the time goes in v1:
time: 38.2 us; the launch traced here: 37.8 us
  blocking collectives  15.1 us (40%)
  starting transfers between devices  10.2 us (27%)
  Pallas kernels  7.96 us (21%)
  between operations  2.45 us (6%)
  waiting for transfers between devices  0.93 us (2%)
  other arithmetic  0.63 us (2%)
  local copies, waits for them, and re-layouts  0.62 us (2%)
    all_to_all x1, blocking collectives, local(): lax.all_to_all(energy, ('grp', 'sub'), split_axis=0, concat_axis=0, tiled...  15.1 us
    all_to_all x1, starting transfers between devices, local(): lax.all_to_all(near, 'sub', split_axis=0, concat_axis=0, tiled=True)  7.41 us
    pallas_call x1, Pallas kernels, local(): pl.pallas_call(inner_kernel, out_shape=(jax.ShapeDtypeStruct((4, VOLUME_N...  3.17 us
    pallas_call x1, Pallas kernels, local(): pl.pallas_call(lambda *refs: outer_kernel(peers, *refs), out_shape=(jax.S...  2.59 us
    pallas_call x1, Pallas kernels, local(): pl.pallas_call(lambda *refs: pack_kernel(peers, *refs), out_shape=(jax.Sh...  2.2 us
    ppermute x1, starting transfers between devices, local(): from_below = lax.ppermute(up, 'grp', [(g, g + 1) for g in range(slabs - 1)])  1.46 us
    ppermute x1, starting transfers between devices, local(): lax.ppermute(down, 'grp', [(g + 1, g) for g in range(slabs - 1)])  1.29 us
    all_to_all x1, waiting for transfers between devices, local(): lax.all_to_all(near, 'sub', split_axis=0, concat_axis=0, tiled=True)  0.77 us
  transfers between devices with their start and end apart: 3, of which 2 were waited for; matrix products, arithmetic and copies ran while one was open for 0% of the time, Pallas kernels for 8%

profile of v1, /device:TPU:0, one launch (start us, length us, event | category | flops | bytes accessed | tf_op | source)
XLA Modules:
  0.0 37.8 jit_solution(167399239056175162)
XLA Ops:
  0.6 2.2 %pack.1 = (f32[8,16,128]{2,1,0:T(8,128)}, f32[16,128]{1,0:T(8,128)}, f32[16,128]{1,0:T(8,128)}) custom-call(f32[35,4,256]{2,1,0:T(4,128)} %bitcast.8, s32[4,256]{1,0:T(4,128)} %refs_3_.1, s32[4,256]{1,0:T(4,128)} %orient_ref.1), custom_call_target="tpu_custom_call" | custom-call | tf_op jit(solution)/shard_map/pack/pallas_call | solution.py:328
  2.8 0.0 copy-start.4
  2.8 0.0 copy-start.3
  2.8 7.4 %all-to-all-start = ((f32[8,16,128]{2,1,0:T(8,128)}), f32[8,16,128]{2,1,0:T(8,128)S(1)}, u32[]{:S(2)}, u32[]{:S(2)}) async-start(f32[8,16,128]{2,1,0:T(8,128)} %get-tuple-element.15), calls=%async_computation | async-start | bytes 131072 | tf_op jit(solution)/shard_map/all_to_all | solution.py:338
  10.2 0.0 copy-done.4
  10.3 1.5 %collective-permute-start = (f32[16,128]{1,0:T(8,128)S(1)}, f32[16,128]{1,0:T(8,128)S(1)}, u32[]{:S(2)}, u32[]{:S(2)}) collective-permute-start(f32[16,128]{1,0:T(8,128)S(1)} %copy-done.4), channel_id=1, source_target_pairs={{0,8},{8,16},{16,24},{1,9},{9,17},{17,25},{2,10},{10,18},{18,26},{... | collective-permute-start | bytes 24584 | tf_op jit(solution)/shard_map/ppermute | solution.py:339
  11.7 0.0 copy-done.3
  11.7 1.3 %collective-permute-start.1 = (f32[16,128]{1,0:T(8,128)S(1)}, f32[16,128]{1,0:T(8,128)S(1)}, u32[]{:S(2)}, u32[]{:S(2)}) collective-permute-start(f32[16,128]{1,0:T(8,128)S(1)} %copy-done.3), channel_id=1, source_target_pairs={{8,0},{16,8},{24,16},{9,1},{17,9},{25,17},{10,2},{18,10},{26,18},{... | collective-permute-start | bytes 24584 | tf_op jit(solution)/shard_map/ppermute | solution.py:340
  13.0 3.2 %inner.1 = (f32[4,35,256]{2,1,0:T(8,128)}, f32[4,35,256]{2,1,0:T(8,128)}, f32[64,256]{1,0:T(8,128)}, f32[4,256]{1,0:T(4,128)}, f32[1,256]{1,0:T(1,128)}, /*index=5*/bf16[35,256]{1,0:T(8,128)(2,1)}) custom-call(f32[35,4,256]{2,1,0:T(4,128)} %bitcast.9, f32[35,4,256]{2,1,0:T(4,128)} %bitcast.10, f32[9,256]{1,0:T(8,128)} %metric_ref.1, f32[3,4,256]{2,1,0:T(4,128)} %bitcast.11, ...), custom_call_target="tpu_custom_call" | custom-call | tf_op jit(solution)/shard_map/inner/pallas_call | solution.py:341
  16.2 0.0 collective-permute-done.refs_1_
  16.2 0.0 copy-start.1
  16.2 0.2 collective-permute-done.1.refs_2_
  16.4 0.0 copy-start.2
  16.4 0.8 %all-to-all-done.refs_0_ = f32[8,16,128]{2,1,0:T(8,128)S(1)} async-done(((f32[8,16,128]{2,1,0:T(8,128)}), f32[8,16,128]{2,1,0:T(8,128)S(1)}, u32[]{:S(2)}, u32[]{:S(2)}) %all-to-all-start) | async-done | bytes 65568 | tf_op jit(solution)/shard_map/all_to_all | solution.py:338
  17.2 0.0 copy-start
  17.2 0.0 copy-done.1
  17.2 0.0 copy-done.2
  17.2 0.6 %copy-done = f32[8,16,128]{2,1,0:T(8,128)} copy-done((f32[8,16,128]{2,1,0:T(8,128)}, f32[8,16,128]{2,1,0:T(8,128)S(1)}, u32[]{:S(2)}) %copy-start) | copy-done | bytes 65560
  17.8 2.6 %outer.1 = (f32[35,4,256]{2,1,0:T(4,128)}, f32[35,4,256]{2,1,0:T(4,128)}, f32[32,1,128]{2,1,0:T(1,128)}) custom-call(f32[8,16,128]{2,1,0:T(8,128)} %copy-done, f32[16,128]{1,0:T(8,128)} %copy-done.1, f32[16,128]{1,0:T(8,128)} %copy-done.2, s32[4,256]{1,0:T(4,128)} %refs_3_.1, f32[3,4,256]{2,1,0:T(4,128)} %bitcast.12, f32[4,256]{1,0:T(4,128)} %get-tuple-element.18.refs_5_, ...), custom_call_target="tpu_custom_call" | custom-call | tf_op jit(solution)/shard_map/outer/pallas_call | solution.py:370
  20.4 15.1 %all_to_all.10 = f32[32,1,128]{2,1,0:T(1,128)S(1)} all-to-all(f32[32,1,128]{2,1,0:T(1,128)} %get-tuple-element.26), channel_id=1, replica_groups=mesh['grp'=4,'sub'=8] {'grp','sub'}, dimensions={0} | all-to-all | bytes 32768 | tf_op jit(solution)/shard_map/all_to_all | solution.py:391
  35.4 0.6 %reduce_sum.9 = f32[]{:T(128)} reduce(f32[32,1,128]{2,1,0:T(1,128)S(1)} %all_to_all.10, f32[]{:T(128)} %constant.1.clone.1), dimensions={0,1,2}, to_apply=%region_0.0 | reduce | flops 4095 | bytes 16392 | tf_op jit(solution)/shard_map/reduce_sum | solution.py:396
Async XLA Ops:
  2.8 7.4 %copy-start.4 = (f32[16,128]{1,0:T(8,128)S(1)}, f32[16,128]{1,0:T(8,128)}, u32[]{:S(2)}) copy-start(f32[16,128]{1,0:T(8,128)} %get-tuple-element.16) | copy-start | bytes 24580
  2.8 8.9 %copy-start.3 = (f32[16,128]{1,0:T(8,128)S(1)}, f32[16,128]{1,0:T(8,128)}, u32[]{:S(2)}) copy-start(f32[16,128]{1,0:T(8,128)} %get-tuple-element.17) | copy-start | bytes 24580
  2.8 14.3 %all-to-all-start = ((f32[8,16,128]{2,1,0:T(8,128)}), f32[8,16,128]{2,1,0:T(8,128)S(1)}, u32[]{:S(2)}, u32[]{:S(2)}) async-start(f32[8,16,128]{2,1,0:T(8,128)} %get-tuple-element.15), calls=%async_computation | async-start | bytes 131072 | tf_op jit(solution)/shard_map/all_to_all | solution.py:338
  10.3 6.0 %collective-permute-start = (f32[16,128]{1,0:T(8,128)S(1)}, f32[16,128]{1,0:T(8,128)S(1)}, u32[]{:S(2)}, u32[]{:S(2)}) collective-permute-start(f32[16,128]{1,0:T(8,128)S(1)} %copy-done.4), channel_id=1, source_target_pairs={{0,8},{8,16},{16,24},{1,9},{9,17},{17,25},{2,10},{10,18},{18,26},{... | collective-permute-start | bytes 24584 | tf_op jit(solution)/shard_map/ppermute | solution.py:339
  11.7 4.7 %collective-permute-start.1 = (f32[16,128]{1,0:T(8,128)S(1)}, f32[16,128]{1,0:T(8,128)S(1)}, u32[]{:S(2)}, u32[]{:S(2)}) collective-permute-start(f32[16,128]{1,0:T(8,128)S(1)} %copy-done.3), channel_id=1, source_target_pairs={{8,0},{16,8},{24,16},{9,1},{17,9},{25,17},{10,2},{18,10},{26,18},{... | collective-permute-start | bytes 24584 | tf_op jit(solution)/shard_map/ppermute | solution.py:340
  16.2 0.9 %copy-start.1 = (f32[16,128]{1,0:T(8,128)}, f32[16,128]{1,0:T(8,128)S(1)}, u32[]{:S(2)}) copy-start(f32[16,128]{1,0:T(8,128)S(1)} %collective-permute-done.refs_1_) | copy-start | bytes 24580
  16.4 0.8 %copy-start.2 = (f32[16,128]{1,0:T(8,128)}, f32[16,128]{1,0:T(8,128)S(1)}, u32[]{:S(2)}) copy-start(f32[16,128]{1,0:T(8,128)S(1)} %collective-permute-done.1.refs_2_) | copy-start | bytes 24580
  17.2 0.6 %copy-start = (f32[8,16,128]{2,1,0:T(8,128)}, f32[8,16,128]{2,1,0:T(8,128)S(1)}, u32[]{:S(2)}) copy-start(f32[8,16,128]{2,1,0:T(8,128)S(1)} %all-to-all-done.refs_0_) | copy-start | bytes 196612

commit v2 on v1

v2 whole, which is shorter than its diff:
```python
import jax
import jax.numpy as jnp
import numpy as np
from jax import lax
from jax.experimental import pallas as pl
from jax.experimental.pallas import tpu as pltpu
from jax.sharding import PartitionSpec as P


VOLUME_NODES = 35
FACE_NODES = 15
ROWS = 16
PITCH = 24
TRACE_PITCH = 72

RUNGE_CARRY = -567301805773.0 / 1357537059087.0
RUNGE_ADVANCE = 5161836677717.0 / 13612068292357.0
TIME_STEP = 0.02
INVERSE_TURN = (0, 2, 1, 3, 4, 5)


def node_tables():
    volume_list = [
        (a, b, c, 4 - a - b - c)
        for a in range(5)
        for b in range(5 - a)
        for c in range(5 - a - b)
    ]
    triples = [(a, b, 4 - a - b) for a in range(5) for b in range(5 - a)]
    face_index = np.zeros((4, 15), np.int32)
    for facet in range(4):
        others = [corner for corner in range(4) if corner != facet]
        for node_pos in range(15):
            corners = [0, 0, 0, 0]
            for place_pos in range(3):
                corners[others[place_pos]] = triples[node_pos][place_pos]
            face_index[facet, node_pos] = volume_list.index(tuple(corners))
    vertex_orders = [(0, 1, 2), (1, 2, 0), (2, 0, 1), (0, 2, 1), (2, 1, 0), (1, 0, 2)]
    turn_index = np.zeros((6, 15), np.int32)
    for option in range(6):
        order = vertex_orders[option]
        for node_pos in range(15):
            triple = triples[node_pos]
            turned = (triple[order[0]], triple[order[1]], triple[order[2]])
            turn_index[option, node_pos] = triples.index(turned)
    return face_index, turn_index


FACE_INDEX, TURN_INDEX = node_tables()


def split_three(value):
    high = value.astype(jnp.bfloat16)
    rest = value - high.astype(jnp.float32)
    middle = rest.astype(jnp.bfloat16)
    low = (rest - middle.astype(jnp.float32)).astype(jnp.bfloat16)
    return high, middle, low


def select_turn(nodes, is_turn, j):
    by_source = {}
    for option in range(6):
        source = int(TURN_INDEX[INVERSE_TURN[option], j])
        by_source.setdefault(source, []).append(option)
    items = list(by_source.items())
    value = nodes[items[0][0]]
    for source, options in items[1:]:
        mask = is_turn[options[0]]
        for option in options[1:]:
            mask = mask | is_turn[option]
        value = jnp.where(mask, nodes[source], value)
    return value


def lane_halves(ref, row):
    halves = [jnp.broadcast_to(ref[row : row + 1, h * 128 : h * 128 + 128], (4, 128)) for h in (0, 1)]
    return jnp.concatenate(halves, 0)


def add_parts(value):
    rows = value.shape[0] // 3
    return value[:rows] + (value[rows : 2 * rows] + value[2 * rows :])


def mark_hits(code_ref, hits_ref):
    elements_here = code_ref.shape[1]
    for facet in range(4):
        codes = code_ref[facet : facet + 1, :] - 4 * elements_here
        rows = lax.broadcasted_iota(jnp.int32, (hits_ref.shape[0], elements_here), 0)
        hits_ref[:, facet * elements_here : (facet + 1) * elements_here] = jnp.where(
            rows == codes, 1.0, 0.0
        ).astype(jnp.bfloat16)


def pack_kernel(peers, count, *refs):
    source = refs[:count]
    near_ref, up_ref, down_ref, parts_ref = refs[2 * count - 1 : 2 * count + 3]
    hits_ref, orient_ref, turned_ref, box_ref, sems, box_sem = refs[2 * count + 3 :]
    target = (refs[count], orient_ref) + refs[count + 1 : 2 * count - 1]
    copies = [pltpu.make_async_copy(source[i], target[i], sems.at[i]) for i in range(count)]
    for copy in copies:
        copy.start()
    code_ref, fields_ref = target[0], target[2]
    elements_here = code_ref.shape[1]
    width = elements_here // 8
    blocks = peers + 2
    copies[0].wait()
    mark_hits(code_ref, hits_ref)
    copies[1].wait()
    copies[2].wait()
    for facet in range(4):
        own_turn = lane_halves(orient_ref, facet)
        is_turn = [own_turn == option for option in range(6)]
        nodes = []
        for j in range(FACE_NODES):
            node = int(FACE_INDEX[facet, j])
            nodes.append(fields_ref[node * 8 : node * 8 + 8, :])
        for j in range(ROWS):
            if j < FACE_NODES:
                value = select_turn(nodes, is_turn, j)
            else:
                value = jnp.zeros((8, 128), jnp.float32)
            turned_ref[facet, pl.ds(j, 8, stride=PITCH), :] = value
    turned = jnp.concatenate(
        [
            jnp.concatenate(
                [turned_ref[f, (h * 4 + c) * PITCH : (h * 4 + c) * PITCH + ROWS, :] for c in range(4)], 0
            )
            for f in range(4)
            for h in range(2)
        ],
        1,
    )
    parts = jnp.concatenate(split_three(turned), 0)
    parts_ref[...] = parts
    packed = add_parts(
        lax.dot_general(
            parts, hits_ref[...], (((1,), (1,)), ((), ())), preferred_element_type=jnp.float32
        )
    )
    for block in range(blocks):
        columns = slice(block * width, (block + 1) * width)
        value = jnp.concatenate(
            [packed[c * ROWS : (c + 1) * ROWS, columns] for c in range(4)], 1
        )
        if block < peers:
            box_ref[block] = value
        elif block == peers:
            down_ref[...] = value
        else:
            up_ref[...] = value
    out = pltpu.make_async_copy(box_ref, near_ref, box_sem)
    out.start()
    for copy in copies[3:]:
        copy.wait()
    out.wait()


def inner_kernel(
    code_ref,
    fields_ref,
    store_ref,
    metric_ref,
    normal_ref,
    scale_ref,
    damping_ref,
    mask_ref,
    level_ref,
    derivative_ref,
    lift_ref,
    parts_ref,
    base_ref,
    plain_ref,
    flux_ref,
    weight_ref,
    absorb_ref,
    lift_out_ref,
    trace_ref,
):
    elements_here = code_ref.shape[1]
    total_faces = 4 * elements_here
    growth = jnp.exp2(level_ref[...].astype(jnp.float32))
    absorb = damping_ref[...] * mask_ref[...].astype(jnp.float32)
    absorb_ref[...] = absorb
    weight = 0.5 * (scale_ref[...] * growth)
    weight_ref[...] = weight

    def by_field(ref, c):
        return jnp.concatenate(
            [ref[pl.ds(h * 4 + c, VOLUME_NODES, stride=8), :] for h in range(2)], 1
        )

    for facet in range(4):
        for j in range(ROWS):
            if j < FACE_NODES:
                node = int(FACE_INDEX[facet, j])
                value = fields_ref[node * 8 : node * 8 + 8, :]
            else:
                value = jnp.zeros((8, 128), jnp.float32)
            trace_ref[pl.ds(facet * ROWS + j, 8, stride=TRACE_PITCH), :] = value
    parts = parts_ref[...]
    for facet in range(4):
        codes = code_ref[facet : facet + 1, :]
        hits = jnp.where(
            lax.broadcasted_iota(jnp.int32, (total_faces, elements_here), 0) == codes, 1.0, 0.0
        ).astype(jnp.bfloat16)
        found = add_parts(jnp.dot(parts, hits, preferred_element_type=jnp.float32))
        inside = []
        for c in range(4):
            starts = [(h * 4 + c) * TRACE_PITCH + facet * ROWS for h in range(2)]
            inside.append(jnp.concatenate([trace_ref[a : a + ROWS, :] for a in starts], 1))
        outside = [found[c * ROWS : (c + 1) * ROWS] for c in range(4)]
        normal = [normal_ref[x, facet : facet + 1, :] for x in range(3)]
        wall = codes < 0
        normal_in = normal[0] * inside[1] + normal[1] * inside[2] + normal[2] * inside[3]
        press_jump = jnp.where(wall, 0.0, inside[0] - outside[0])
        normal_jump = jnp.zeros_like(press_jump)
        for x in range(3):
            step = jnp.where(wall, 2.0 * normal[x] * normal_in, inside[1 + x] - outside[1 + x])
            normal_jump = normal_jump + normal[x] * step
        flux_ref[facet * ROWS : (facet + 1) * ROWS, :] = weight[facet : facet + 1] * (
            normal_jump - press_jump
        )
    plain = [by_field(fields_ref, c) for c in range(4)]
    for c in range(4):
        plain_ref[c] = plain[c]
    joined = jnp.concatenate(plain, 1)
    padded = jnp.concatenate([joined, jnp.zeros((5, joined.shape[1]), jnp.float32)], 0)
    high = padded.astype(jnp.bfloat16).astype(jnp.float32)
    stacked = jnp.concatenate([high, padded - high, high], 0).astype(jnp.bfloat16)
    slopes = []
    gap = jnp.zeros((VOLUME_NODES, 5), jnp.float32)
    for y in range(3):
        whole = derivative_ref[y]
        lead = whole.astype(jnp.bfloat16).astype(jnp.float32)
        left = jnp.concatenate([lead, gap, lead, gap, whole - lead, gap], 1).astype(jnp.bfloat16)
        slopes.append(jnp.dot(left, stacked, preferred_element_type=jnp.float32))

    def slope(y, c):
        return slopes[y][:, c * elements_here : (c + 1) * elements_here]

    metric = metric_ref[...] * growth

    def physical(x, c):
        total = metric[3 * x : 3 * x + 1] * slope(0, c)
        for y in (1, 2):
            total = total + metric[3 * x + y : 3 * x + y + 1] * slope(y, c)
        return total

    for c in range(4):
        if c == 0:
            volume = physical(0, 1) + physical(1, 2) + physical(2, 3)
        else:
            volume = physical(c - 1, 0)
        change = -volume - absorb * plain[c]
        base_ref[c] = RUNGE_CARRY * by_field(store_ref, c) + TIME_STEP * change
    none = jnp.zeros((VOLUME_NODES, 1), jnp.float32)
    pieces = []
    for facet in range(4):
        pieces += [lift_ref[:, facet * FACE_NODES : (facet + 1) * FACE_NODES], none]
    high, middle, _ = split_three(jnp.concatenate(pieces, 1))
    lift_out_ref[...] = jnp.concatenate([high, high, middle, middle], 1)


def outer_kernel(
    peers,
    hold_hits,
    near_ref,
    below_ref,
    above_ref,
    hits_ref,
    normal_ref,
    weight_ref,
    flux_ref,
    lift_ref,
    base_ref,
    plain_ref,
    absorb_ref,
    fields_ref,
    store_ref,
    energy_ref,
    *scratch,
):
    elements_here = plain_ref.shape[2]
    width = elements_here // 8
    if not hold_hits:
        mark_hits(hits_ref, scratch[0])
        hits_ref = scratch[0]
    boxes = [near_ref[block] for block in range(peers)] + [below_ref[...], above_ref[...]]
    received = jnp.concatenate(
        [
            jnp.concatenate([box[:, c * width : (c + 1) * width] for box in boxes], 1)
            for c in range(4)
        ],
        0,
    )
    parts = jnp.concatenate(split_three(received), 0)
    found = add_parts(jnp.dot(parts, hits_ref[...], preferred_element_type=jnp.float32))
    pieces = []
    for facet in range(4):
        columns = slice(facet * elements_here, (facet + 1) * elements_here)
        outside = [found[c * ROWS : (c + 1) * ROWS, columns] for c in range(4)]
        normal = [normal_ref[x, facet : facet + 1, :] for x in range(3)]
        across = normal[0] * outside[1] + normal[1] * outside[2] + normal[2] * outside[3]
        weight = weight_ref[facet : facet + 1, :]
        press = flux_ref[facet * ROWS : (facet + 1) * ROWS, :] + weight * (outside[0] - across)
        pieces.append([press] + [-normal[x] * press for x in range(3)])
    flux = jnp.concatenate(
        [jnp.concatenate([pieces[facet][c] for facet in range(4)], 0) for c in range(4)], 1
    )
    high = flux.astype(jnp.bfloat16)
    middle = (flux - high.astype(jnp.float32)).astype(jnp.bfloat16)
    lifted = jnp.dot(
        lift_ref[...],
        jnp.concatenate([high, middle, high, middle], 0),
        preferred_element_type=jnp.float32,
    )
    square = jnp.zeros((VOLUME_NODES, elements_here), jnp.float32)
    for c in range(4):
        columns = slice(c * elements_here, (c + 1) * elements_here)
        store_next = base_ref[c] + TIME_STEP * lifted[:, columns]
        fields_next = plain_ref[c] + RUNGE_ADVANCE * store_next
        for h in range(2):
            lanes = slice(h * 128, h * 128 + 128)
            store_ref[pl.ds(h * 4 + c, VOLUME_NODES, stride=8), :] = store_next[:, lanes]
            fields_ref[pl.ds(h * 4 + c, VOLUME_NODES, stride=8), :] = fields_next[:, lanes]
        square = square + fields_next * fields_next
    energy = jnp.sum(square, 0, keepdims=True) * absorb_ref[...]
    total = energy[:, :128] + energy[:, 128:]
    energy_ref[...] = jnp.broadcast_to(total[None], energy_ref.shape)


def finish_kernel(divisor, shares_ref, fields_in, store_in, total_ref, fields_out, store_out, sems):
    one = pltpu.make_async_copy(fields_in, fields_out, sems.at[0])
    two = pltpu.make_async_copy(store_in, store_out, sems.at[1])
    one.start()
    two.start()
    total_ref[0] = jnp.sum(shares_ref[...]) * (1.0 / divisor)
    one.wait()
    two.wait()


def as_rows(value):
    fields, nodes, elements = value.shape
    value = jnp.transpose(value.reshape(fields, nodes, elements // 128, 128), (1, 2, 0, 3))
    return value.reshape(nodes * 8, 128)


def from_rows(value, nodes):
    value = jnp.transpose(value.reshape(nodes, 2, 4, 128), (2, 0, 1, 3))
    return value.reshape(4, nodes, 256)


def in_vmem(*values):
    return [pltpu.with_memory_space_constraint(value, pltpu.VMEM) for value in values]


def local(
    fields,
    section_store,
    metric_terms,
    normals,
    face_scale,
    damping,
    absorb_mask,
    refine_level,
    face_source,
    orientation,
    derivative,
    lift_matrix,
):
    elements_here = fields.shape[2]
    assert elements_here == 256
    total_faces = 4 * elements_here
    peers = lax.axis_size("sub")
    slabs = lax.axis_size("grp")
    devices = peers * slabs
    slots = (peers + 2) * (elements_here // 8)
    f32 = jnp.float32
    bf16 = jnp.bfloat16
    hits_shape = pltpu.VMEM((slots, total_faces), bf16)
    hold_hits = 2 * slots * total_faces <= 2**20
    row = (1, elements_here)
    given = [
        face_source,
        orientation,
        as_rows(fields),
        as_rows(section_store),
        metric_terms,
        jnp.transpose(normals, (1, 0, 2)),
        face_scale,
        damping.reshape(row),
        absorb_mask.reshape(row),
        refine_level.reshape(row),
        derivative,
        lift_matrix,
    ]
    count = len(given)
    kept = given[:1] + given[2:]
    packed = pl.pallas_call(
        lambda *refs: pack_kernel(peers, count, *refs),
        out_shape=tuple(pltpu.VMEM(value.shape, value.dtype) for value in kept)
        + (
            jax.ShapeDtypeStruct((peers, ROWS, 128), f32),
            pltpu.VMEM((ROWS, 128), f32),
            pltpu.VMEM((ROWS, 128), f32),
            pltpu.VMEM((12 * ROWS, total_faces), bf16),
        )
        + ((hits_shape,) if hold_hits else ()),
        in_specs=[pl.BlockSpec(memory_space=pltpu.HBM)] * count,
        out_specs=tuple([pl.BlockSpec(memory_space=pltpu.VMEM)] * len(kept))
        + (pl.BlockSpec(memory_space=pltpu.HBM),)
        + tuple([pl.BlockSpec(memory_space=pltpu.VMEM)] * (4 if hold_hits else 3)),
        scratch_shapes=([] if hold_hits else [hits_shape])
        + [
            pltpu.VMEM((4, elements_here), jnp.int32),
            pltpu.VMEM((4, 8 * PITCH, 128), f32),
            pltpu.VMEM((peers, ROWS, 128), f32),
            pltpu.SemaphoreType.DMA((count,)),
            pltpu.SemaphoreType.DMA,
        ],
        name="pack",
    )(*given)
    held = packed[: len(kept)]
    near, up, down, parts = packed[len(kept) : len(kept) + 4]
    first = [(g, g + 1) for g in range(0, slabs - 1, 2)]
    second = [(g, g + 1) for g in range(1, slabs - 1, 2)]
    odd = lax.axis_index("grp") % 2 == 1
    arrived = lax.all_to_all(near, "sub", split_axis=0, concat_axis=0, tiled=True)
    swap_a = lax.ppermute(jnp.where(odd, down, up), "grp", first + [(b, a) for a, b in first])
    swap_b = lax.ppermute(jnp.where(odd, up, down), "grp", second + [(b, a) for a, b in second])
    from_below = jnp.where(odd, swap_a, swap_b)
    from_above = jnp.where(odd, swap_b, swap_a)
    base, plain, flux, weight, absorb, lift_parts = pl.pallas_call(
        inner_kernel,
        out_shape=(
            pltpu.VMEM((4, VOLUME_NODES, elements_here), f32),
            pltpu.VMEM((4, VOLUME_NODES, elements_here), f32),
            pltpu.VMEM((4 * ROWS, elements_here), f32),
            pltpu.VMEM((4, elements_here), f32),
            pltpu.VMEM(row, f32),
            pltpu.VMEM((VOLUME_NODES, 16 * ROWS), bf16),
        ),
        scratch_shapes=[pltpu.VMEM((8 * TRACE_PITCH, 128), f32)],
        name="inner",
    )(*in_vmem(*held, parts))
    fields_next, store_next, energy = pl.pallas_call(
        lambda *refs: outer_kernel(peers, hold_hits, *refs),
        out_shape=(
            pltpu.VMEM((VOLUME_NODES * 8, 128), f32),
            pltpu.VMEM((VOLUME_NODES * 8, 128), f32),
            pltpu.VMEM((devices, 1, 128), f32),
        ),
        scratch_shapes=[] if hold_hits else [hits_shape],
        name="outer",
    )(
        *in_vmem(
            arrived,
            from_below,
            from_above,
            packed[-1] if hold_hits else held[0],
            held[4],
            weight,
            flux,
            lift_parts,
            base,
            plain,
            absorb,
        )
    )
    shares = lax.all_to_all(energy, ("grp", "sub"), split_axis=0, concat_axis=0, tiled=True)
    divisor = elements_here * devices * VOLUME_NODES
    total, fields_next, store_next = pl.pallas_call(
        lambda *refs: finish_kernel(divisor, *refs),
        out_shape=(
            jax.ShapeDtypeStruct((1,), f32),
            jax.ShapeDtypeStruct((VOLUME_NODES * 8, 128), f32),
            jax.ShapeDtypeStruct((VOLUME_NODES * 8, 128), f32),
        ),
        in_specs=[pl.BlockSpec(memory_space=pltpu.VMEM)] * 3,
        out_specs=(
            pl.BlockSpec(memory_space=pltpu.SMEM),
            pl.BlockSpec(memory_space=pltpu.HBM),
            pl.BlockSpec(memory_space=pltpu.HBM),
        ),
        scratch_shapes=[pltpu.SemaphoreType.DMA((2,))],
        name="finish",
    )(*in_vmem(shares, fields_next, store_next))
    return (
        from_rows(fields_next, VOLUME_NODES),
        from_rows(store_next, VOLUME_NODES),
        total[0],
    )


def solution(mesh):
    placed = (
        P(None, None, ("grp", "sub")),
        P(None, None, ("grp", "sub")),
        P(None, ("grp", "sub")),
        P(None, None, ("grp", "sub")),
        P(None, ("grp", "sub")),
        P(("grp", "sub")),
        P(("grp", "sub")),
        P(("grp", "sub")),
        P(None, ("grp", "sub")),
        P(None, ("grp", "sub")),
        P(),
        P(),
    )
    return jax.shard_map(
        local,
        mesh=mesh,
        in_specs=placed,
        out_specs=(P(None, None, ("grp", "sub")), P(None, None, ("grp", "sub")), P()),
        check_vma=False,
    )
```

time: 38.2 us -> 31.8 us (0.83)
  blocking collectives: 15.1 us -> 8.84 us
  waiting for transfers between devices: 0.93 us -> 6.04 us
  Pallas kernels: 7.96 us -> 5.04 us
  between operations: 2.45 us -> 0.71 us
  starting transfers between devices: 10.2 us -> 10.9 us
  other arithmetic: 0.63 us -> 0.01 us
  local copies, waits for them, and re-layouts: 0.62 us -> 0 us
    all_to_all x1, blocking collectives: 15.1 us -> 8.84 us  [local(): lax.all_to_all(energy, ('grp', 'sub'), split_axis=0, concat_axis=0, tiled...]
    all_to_all x1, waiting for transfers between devices: 0.77 us -> 6.03 us  [local(): lax.all_to_all(near, 'sub', split_axis=0, concat_axis=0, tiled=True)]
    pallas_call x3 -> x4, Pallas kernels: 7.96 us -> 5.04 us  [the longest x1 2.28 us: local(): pl.pallas_call(lambda *refs: pack_kernel(peers, count, *refs), out_shape=...]
    ppermute x2, starting transfers between devices: 2.75 us -> 5.08 us  [the longest x1 4.42 us: local(): lax.ppermute(jnp.where(odd, down, up), 'grp', first + [(b, a) for a, b in...]
    all_to_all x1, starting transfers between devices: 7.41 us -> 5.81 us  [local(): lax.all_to_all(near, 'sub', split_axis=0, concat_axis=0, tiled=True)]
    reduce_sum x1 -> x0, other arithmetic: 0.63 us -> none  [local(): jnp.sum(shares) / divisor]
    unnamed x10 -> x0, local copies, waits for them, and re-layouts: 0.62 us -> none
  transfers between devices with their start and end apart: 3 -> 3, of which waited for: 2 -> 1; matrix products, arithmetic and copies ran while one was open for 0% -> 0% of each run, Pallas kernels for 8% -> 3%
where the time goes in v2:
time: 31.8 us; the launch traced here: 31.5 us
  starting transfers between devices  10.9 us (34%)
  blocking collectives  8.84 us (28%)
  waiting for transfers between devices  6.04 us (19%)
  Pallas kernels  5.04 us (16%)
  between operations  0.71 us (2%)
    all_to_all x1, blocking collectives, local(): lax.all_to_all(energy, ('grp', 'sub'), split_axis=0, concat_axis=0, tiled...  8.84 us
    all_to_all x1, waiting for transfers between devices, local(): lax.all_to_all(near, 'sub', split_axis=0, concat_axis=0, tiled=True)  6.03 us
    all_to_all x1, starting transfers between devices, local(): lax.all_to_all(near, 'sub', split_axis=0, concat_axis=0, tiled=True)  5.81 us
    ppermute x1, starting transfers between devices, local(): lax.ppermute(jnp.where(odd, down, up), 'grp', first + [(b, a) for a, b in...  4.42 us
    pallas_call x1, Pallas kernels, local(): pl.pallas_call(lambda *refs: pack_kernel(peers, count, *refs), out_shape=...  2.28 us
    pallas_call x1, Pallas kernels, local(): pl.pallas_call(lambda *refs: finish_kernel(divisor, *refs), out_shape=(ja...  1.25 us
    pallas_call x1, Pallas kernels, local(): pl.pallas_call(inner_kernel, out_shape=(pltpu.VMEM((4, VOLUME_NODES, elem...  0.83 us
    pallas_call x1, Pallas kernels, local(): pl.pallas_call(lambda *refs: outer_kernel(peers, hold_hits, *refs), out_s...  0.69 us
  transfers between devices with their start and end apart: 3, of which 1 were waited for; matrix products, arithmetic and copies ran while one was open for 0% of the time, Pallas kernels for 3%

profile of v2, /device:TPU:0, one launch (start us, length us, event | category | flops | bytes accessed | tf_op | source)
XLA Modules:
  0.0 31.5 jit_solution(6821664310626880500)
XLA Ops:
  0.6 2.3 %pack.1 = (s32[4,256]{1,0:T(4,128)S(1)}, f32[280,128]{1,0:T(8,128)S(1)}, f32[280,128]{1,0:T(8,128)S(1)}, f32[9,256]{1,0:T(8,128)S(1)}, f32[3,4,256]{2,1,0:T(4,12...) custom-call(s32[4,256]{1,0:T(4,128)} %refs_0_.1, ...), custom_call_target="tpu_custom_call" | custom-call | tf_op jit(solution)/shard_map/pack/pallas_call | solution.py:400
  2.9 0.7 %collective-permute-start.1 = (f32[16,128]{1,0:T(8,128)S(1)}, f32[16,128]{1,0:T(8,128)S(1)}, u32[]{:S(2)}, u32[]{:S(2)}) collective-permute-start(f32[16,128]{1,0:T(8,128)S(1)} %get-tuple-element.61), channel_id=1, source_target_pairs={{8,16},{16,8},{9,17},{17,9},{10,18},{18,10},{11,19},{19,11},{12,20... | collective-permute-start | bytes 24584 | tf_op jit(solution)/shard_map/ppermute | solution.py:431
  3.6 4.4 %collective-permute-start = (f32[16,128]{1,0:T(8,128)S(1)}, f32[16,128]{1,0:T(8,128)S(1)}, u32[]{:S(2)}, u32[]{:S(2)}) collective-permute-start(f32[16,128]{1,0:T(8,128)S(1)} %get-tuple-element.62), channel_id=1, source_target_pairs={{0,8},{16,24},{8,0},{24,16},{1,9},{17,25},{9,1},{25,17},{2,10},{18... | collective-permute-start | bytes 24584 | tf_op jit(solution)/shard_map/ppermute | solution.py:430
  8.0 5.8 %all-to-all-start = ((f32[8,16,128]{2,1,0:T(8,128)}), f32[8,16,128]{2,1,0:T(8,128)S(1)}, u32[]{:S(2)}, u32[]{:S(2)}) async-start(f32[8,16,128]{2,1,0:T(8,128)} %get-tuple-element.31), calls=%async_computation | async-start | bytes 131072 | tf_op jit(solution)/shard_map/all_to_all | solution.py:429
  13.8 0.8 %inner.1 = (f32[4,35,256]{2,1,0:T(8,128)S(1)}, f32[4,35,256]{2,1,0:T(8,128)S(1)}, f32[64,256]{1,0:T(8,128)S(1)}, f32[4,256]{1,0:T(4,128)S(1)}, f32[1,256]{1,0:T(1,128)S(1)}, /*index=5*/bf16[35,256]{1,0:T(8,128)(2,1)S(1)}) custom-call(s32[4,256]{1,0:T(4,128)S(1)} %get-tuple-element.36.code_ref, f32[280,128]{1,0:T(8,128)S(1)} %get-tuple-element.37.fields_ref, ...), custom_call_target="tpu_custom_call" | custom-call | tf_op jit(solution)/shard_map/inner/pallas_call | solution.py:434
  14.7 0.0 collective-permute-done.1
  14.7 0.0 collective-permute-done
  14.7 6.0 %all-to-all-done.refs_0_ = f32[8,16,128]{2,1,0:T(8,128)S(1)} async-done(((f32[8,16,128]{2,1,0:T(8,128)}), f32[8,16,128]{2,1,0:T(8,128)S(1)}, u32[]{:S(2)}, u32[]{:S(2)}) %all-to-all-start) | async-done | bytes 65568 | tf_op jit(solution)/shard_map/all_to_all | solution.py:429
  20.7 0.7 %outer.1 = (f32[280,128]{1,0:T(8,128)S(1)}, f32[280,128]{1,0:T(8,128)S(1)}, f32[32,1,128]{2,1,0:T(1,128)S(1)}) custom-call(f32[8,16,128]{2,1,0:T(8,128)S(1)} %all-to-all-done.refs_0_, f32[16,128]{1,0:T(8,128)S(1)} %get-tuple-element.60.refs_1_, f32[16,128]{1,0:T(8,128)S(1)} %get-tuple-element.59.refs_2_, bf16[320,1024]{1,0:T(8,128)(2,1)S(1)} %get-tuple-element.34.refs_3_, ...), custom_call_target="tpu_custom_call" | custom-call | tf_op jit(solution)/shard_map/outer/pallas_call | solution.py:447
  21.4 8.8 %all_to_all.10.refs_0_ = f32[32,1,128]{2,1,0:T(1,128)S(1)} all-to-all(f32[32,1,128]{2,1,0:T(1,128)S(1)} %get-tuple-element.53), channel_id=1, replica_groups=mesh['grp'=4,'sub'=8] {'grp','sub'}, dimensions={0} | all-to-all | bytes 32768 | tf_op jit(solution)/shard_map/all_to_all | solution.py:471
  30.3 1.2 %finish.1 = (f32[1]{0:T(128)}, f32[280,128]{1,0:T(8,128)}, f32[280,128]{1,0:T(8,128)}) custom-call(f32[32,1,128]{2,1,0:T(1,128)S(1)} %all_to_all.10.refs_0_, f32[280,128]{1,0:T(8,128)S(1)} %get-tuple-element.54.refs_1_, f32[280,128]{1,0:T(8,128)S(1)} %get-tuple-element.55.refs_2_), custom_call_target="tpu_custom_call" | custom-call | tf_op jit(solution)/shard_map/finish/pallas_call | solution.py:473
  (2 shorter events, 0.0 us)
Async XLA Ops:
  2.9 11.7 %collective-permute-start.1 = (f32[16,128]{1,0:T(8,128)S(1)}, f32[16,128]{1,0:T(8,128)S(1)}, u32[]{:S(2)}, u32[]{:S(2)}) collective-permute-start(f32[16,128]{1,0:T(8,128)S(1)} %get-tuple-element.61), channel_id=1, source_target_pairs={{8,16},{16,8},{9,17},{17,9},{10,18},{18,10},{11,19},{19,11},{12,20... | collective-permute-start | bytes 24584 | tf_op jit(solution)/shard_map/ppermute | solution.py:431
  3.6 11.1 %collective-permute-start = (f32[16,128]{1,0:T(8,128)S(1)}, f32[16,128]{1,0:T(8,128)S(1)}, u32[]{:S(2)}, u32[]{:S(2)}) collective-permute-start(f32[16,128]{1,0:T(8,128)S(1)} %get-tuple-element.62), channel_id=1, source_target_pairs={{0,8},{16,24},{8,0},{24,16},{1,9},{17,25},{9,1},{25,17},{2,10},{18... | collective-permute-start | bytes 24584 | tf_op jit(solution)/shard_map/ppermute | solution.py:430
  8.0 12.7 %all-to-all-start = ((f32[8,16,128]{2,1,0:T(8,128)}), f32[8,16,128]{2,1,0:T(8,128)S(1)}, u32[]{:S(2)}, u32[]{:S(2)}) async-start(f32[8,16,128]{2,1,0:T(8,128)} %get-tuple-element.31), calls=%async_computation | async-start | bytes 131072 | tf_op jit(solution)/shard_map/all_to_all | solution.py:429

commit v3 on v2

--- a/solution.py
+++ b/solution.py
@@ -49,12 +49,9 @@
 FACE_INDEX, TURN_INDEX = node_tables()
 
 
-def split_three(value):
+def split_two(value):
     high = value.astype(jnp.bfloat16)
-    rest = value - high.astype(jnp.float32)
-    middle = rest.astype(jnp.bfloat16)
-    low = (rest - middle.astype(jnp.float32)).astype(jnp.bfloat16)
-    return high, middle, low
+    return high, (value - high.astype(jnp.float32)).astype(jnp.bfloat16)
 
 
 def select_turn(nodes, is_turn, j):
@@ -78,8 +75,8 @@
 
 
 def add_parts(value):
-    rows = value.shape[0] // 3
-    return value[:rows] + (value[rows : 2 * rows] + value[2 * rows :])
+    rows = value.shape[0] // 2
+    return value[:rows] + value[rows:]
 
 
 def mark_hits(code_ref, hits_ref):
@@ -92,7 +89,8 @@
         ).astype(jnp.bfloat16)
 
 
-def pack_kernel(peers, count, *refs):
+def pack_kernel(place, count, *refs):
+    peers = len(place)
     source = refs[:count]
     near_ref, up_ref, down_ref, parts_ref = refs[2 * count - 1 : 2 * count + 3]
     hits_ref, orient_ref, turned_ref, box_ref, sems, box_sem = refs[2 * count + 3 :]
@@ -131,7 +129,7 @@
         ],
         1,
     )
-    parts = jnp.concatenate(split_three(turned), 0)
+    parts = jnp.concatenate(split_two(turned), 0)
     parts_ref[...] = parts
     packed = add_parts(
         lax.dot_general(
@@ -144,7 +142,7 @@
             [packed[c * ROWS : (c + 1) * ROWS, columns] for c in range(4)], 1
         )
         if block < peers:
-            box_ref[block] = value
+            box_ref[place[block]] = value
         elif block == peers:
             down_ref[...] = value
         else:
@@ -258,12 +256,12 @@
     pieces = []
     for facet in range(4):
         pieces += [lift_ref[:, facet * FACE_NODES : (facet + 1) * FACE_NODES], none]
-    high, middle, _ = split_three(jnp.concatenate(pieces, 1))
+    high, middle = split_two(jnp.concatenate(pieces, 1))
     lift_out_ref[...] = jnp.concatenate([high, high, middle, middle], 1)
 
 
 def outer_kernel(
-    peers,
+    place,
     hold_hits,
     near_ref,
     below_ref,
@@ -286,7 +284,7 @@
     if not hold_hits:
         mark_hits(hits_ref, scratch[0])
         hits_ref = scratch[0]
-    boxes = [near_ref[block] for block in range(peers)] + [below_ref[...], above_ref[...]]
+    boxes = [near_ref[p] for p in place] + [below_ref[...], above_ref[...]]
     received = jnp.concatenate(
         [
             jnp.concatenate([box[:, c * width : (c + 1) * width] for box in boxes], 1)
@@ -294,7 +292,7 @@
         ],
         0,
     )
-    parts = jnp.concatenate(split_three(received), 0)
+    parts = jnp.concatenate(split_two(received), 0)
     found = add_parts(jnp.dot(parts, hits_ref[...], preferred_element_type=jnp.float32))
     pieces = []
     for facet in range(4):
@@ -308,8 +306,7 @@
     flux = jnp.concatenate(
         [jnp.concatenate([pieces[facet][c] for facet in range(4)], 0) for c in range(4)], 1
     )
-    high = flux.astype(jnp.bfloat16)
-    middle = (flux - high.astype(jnp.float32)).astype(jnp.bfloat16)
+    high, middle = split_two(flux)
     lifted = jnp.dot(
         lift_ref[...],
         jnp.concatenate([high, middle, high, middle], 0),
@@ -330,14 +327,30 @@
     energy_ref[...] = jnp.broadcast_to(total[None], energy_ref.shape)
 
 
-def finish_kernel(divisor, shares_ref, fields_in, store_in, total_ref, fields_out, store_out, sems):
+def finish_kernel(
+    divisor, shares_ref, fields_in, store_in, total_out, fields_out, store_out, total_ref, sems
+):
     one = pltpu.make_async_copy(fields_in, fields_out, sems.at[0])
     two = pltpu.make_async_copy(store_in, store_out, sems.at[1])
+    three = pltpu.make_async_copy(total_ref, total_out, sems.at[2])
     one.start()
     two.start()
     total_ref[0] = jnp.sum(shares_ref[...]) * (1.0 / divisor)
+    three.start()
     one.wait()
     two.wait()
+    three.wait()
+
+
+def group_order(peers):
+    lead = max(peers // 2 - 1, 0)
+    rest = [member for member in range(peers) if member != lead]
+    order = [lead]
+    while rest:
+        order.append(rest.pop())
+        if rest:
+            order.append(rest.pop(0))
+    return order, [order.index(member) for member in range(peers)]
 
 
 def as_rows(value):
@@ -374,6 +387,7 @@
     total_faces = 4 * elements_here
     peers = lax.axis_size("sub")
     slabs = lax.axis_size("grp")
+    order, place = group_order(peers)
     devices = peers * slabs
     slots = (peers + 2) * (elements_here // 8)
     f32 = jnp.float32
@@ -398,13 +412,13 @@
     count = len(given)
     kept = given[:1] + given[2:]
     packed = pl.pallas_call(
-        lambda *refs: pack_kernel(peers, count, *refs),
+        lambda *refs: pack_kernel(place, count, *refs),
         out_shape=tuple(pltpu.VMEM(value.shape, value.dtype) for value in kept)
         + (
             jax.ShapeDtypeStruct((peers, ROWS, 128), f32),
             pltpu.VMEM((ROWS, 128), f32),
             pltpu.VMEM((ROWS, 128), f32),
-            pltpu.VMEM((12 * ROWS, total_faces), bf16),
+            pltpu.VMEM((8 * ROWS, total_faces), bf16),
         )
         + ((hits_shape,) if hold_hits else ()),
         in_specs=[pl.BlockSpec(memory_space=pltpu.HBM)] * count,
@@ -424,9 +438,12 @@
     held = packed[: len(kept)]
     near, up, down, parts = packed[len(kept) : len(kept) + 4]
     first = [(g, g + 1) for g in range(0, slabs - 1, 2)]
-    second = [(g, g + 1) for g in range(1, slabs - 1, 2)]
+    second = [(g, (g + 1) % slabs) for g in range(1, slabs, 2)]
+    second = [pair for pair in second if slabs % 2 == 0 or pair[1] > 0]
     odd = lax.axis_index("grp") % 2 == 1
-    arrived = lax.all_to_all(near, "sub", split_axis=0, concat_axis=0, tiled=True)
+    arrived = lax.all_to_all(
+        near, "sub", split_axis=0, concat_axis=0, tiled=True, axis_index_groups=[order]
+    )
     swap_a = lax.ppermute(jnp.where(odd, down, up), "grp", first + [(b, a) for a, b in first])
     swap_b = lax.ppermute(jnp.where(odd, up, down), "grp", second + [(b, a) for a, b in second])
     from_below = jnp.where(odd, swap_a, swap_b)
@@ -445,7 +462,7 @@
         name="inner",
     )(*in_vmem(*held, parts))
     fields_next, store_next, energy = pl.pallas_call(
-        lambda *refs: outer_kernel(peers, hold_hits, *refs),
+        lambda *refs: outer_kernel(place, hold_hits, *refs),
         out_shape=(
             pltpu.VMEM((VOLUME_NODES * 8, 128), f32),
             pltpu.VMEM((VOLUME_NODES * 8, 128), f32),
@@ -479,11 +496,11 @@
         ),
         in_specs=[pl.BlockSpec(memory_space=pltpu.VMEM)] * 3,
         out_specs=(
-            pl.BlockSpec(memory_space=pltpu.SMEM),
+            pl.BlockSpec(memory_space=pltpu.HBM),
             pl.BlockSpec(memory_space=pltpu.HBM),
             pl.BlockSpec(memory_space=pltpu.HBM),
         ),
-        scratch_shapes=[pltpu.SemaphoreType.DMA((2,))],
+        scratch_shapes=[pltpu.SMEM((1,), f32), pltpu.SemaphoreType.DMA((3,))],
         name="finish",
     )(*in_vmem(shares, fields_next, store_next))
     return (

time: 31.8 us -> 27.9 us (0.88)
  waiting for transfers between devices: 6.04 us -> 3.82 us
  starting transfers between devices: 10.9 us -> 9.54 us
  Pallas kernels: 5.04 us -> 4.25 us
  blocking collectives: 8.84 us -> 9.33 us
    ppermute x1, starting transfers between devices: 4.42 us -> 0.68 us  [local(): lax.ppermute(jnp.where(odd, down, up), 'grp', first + [(b, a) for a, b in...]
    all_to_all x1, waiting for transfers between devices: 6.03 us -> 3.82 us  [local(): lax.all_to_all(near, 'sub', split_axis=0, concat_axis=0, tiled=True, axis...]
    ppermute x1, starting transfers between devices: 0.66 us -> 2.5 us  [local(): lax.ppermute(jnp.where(odd, up, down), 'grp', second + [(b, a) for a, b i...]
    all_to_all x1, starting transfers between devices: 5.81 us -> 6.37 us  [local(): lax.all_to_all(near, 'sub', split_axis=0, concat_axis=0, tiled=True, axis...]
    pallas_call x1, Pallas kernels: 1.25 us -> 0.75 us  [local(): pl.pallas_call(lambda *refs: finish_kernel(divisor, *refs), out_shape=(ja...]
    all_to_all x1, blocking collectives: 8.84 us -> 9.33 us  [local(): lax.all_to_all(energy, ('grp', 'sub'), split_axis=0, concat_axis=0, tiled...]
  transfers between devices with their start and end apart: 3 -> 3, of which waited for: 1 -> 1; matrix products, arithmetic and copies ran while one was open for 0% -> 0% of each run, Pallas kernels for 3% -> 2%
where the time goes in v3:
time: 27.9 us; the launch traced here: 27.7 us
  starting transfers between devices  9.54 us (34%)
  blocking collectives  9.33 us (33%)
  Pallas kernels  4.25 us (15%)
  waiting for transfers between devices  3.82 us (14%)
  between operations  0.7 us (3%)
    all_to_all x1, blocking collectives, local(): lax.all_to_all(energy, ('grp', 'sub'), split_axis=0, concat_axis=0, tiled...  9.33 us
    all_to_all x1, starting transfers between devices, local(): lax.all_to_all(near, 'sub', split_axis=0, concat_axis=0, tiled=True, axis...  6.37 us
    all_to_all x1, waiting for transfers between devices, local(): lax.all_to_all(near, 'sub', split_axis=0, concat_axis=0, tiled=True, axis...  3.82 us
    ppermute x1, starting transfers between devices, local(): lax.ppermute(jnp.where(odd, up, down), 'grp', second + [(b, a) for a, b i...  2.5 us
    pallas_call x1, Pallas kernels, local(): pl.pallas_call(lambda *refs: pack_kernel(place, count, *refs), out_shape=...  2.2 us
    pallas_call x1, Pallas kernels, local(): pl.pallas_call(lambda *refs: finish_kernel(divisor, *refs), out_shape=(ja...  0.75 us
    pallas_call x1, Pallas kernels, local(): pl.pallas_call(inner_kernel, out_shape=(pltpu.VMEM((4, VOLUME_NODES, elem...  0.68 us
    ppermute x1, starting transfers between devices, local(): lax.ppermute(jnp.where(odd, down, up), 'grp', first + [(b, a) for a, b in...  0.68 us
  transfers between devices with their start and end apart: 3, of which 1 were waited for; matrix products, arithmetic and copies ran while one was open for 0% of the time, Pallas kernels for 2%

profile of v3, /device:TPU:0, one launch (start us, length us, event | category | flops | bytes accessed | tf_op | source)
XLA Modules:
  0.0 27.7 jit_solution(10798535392461994137)
XLA Ops:
  0.6 2.2 %pack.1 = (s32[4,256]{1,0:T(4,128)S(1)}, f32[280,128]{1,0:T(8,128)S(1)}, f32[280,128]{1,0:T(8,128)S(1)}, f32[9,256]{1,0:T(8,128)S(1)}, f32[3,4,256]{2,1,0:T(4,12...) custom-call(s32[4,256]{1,0:T(4,128)} %refs_0_.1, ...), custom_call_target="tpu_custom_call" | custom-call | tf_op jit(solution)/shard_map/pack/pallas_call | solution.py:414
  2.9 2.5 %collective-permute-start.1 = (f32[16,128]{1,0:T(8,128)S(1)}, f32[16,128]{1,0:T(8,128)S(1)}, u32[]{:S(2)}, u32[]{:S(2)}) collective-permute-start(f32[16,128]{1,0:T(8,128)S(1)} %get-tuple-element.61), channel_id=1, source_target_pairs={{8,16},{24,0},{16,8},{0,24},{9,17},{25,1},{17,9},{1,25},{10,18},{2... | collective-permute-start | bytes 24584 | tf_op jit(solution)/shard_map/ppermute | solution.py:448
  5.4 0.7 %collective-permute-start = (f32[16,128]{1,0:T(8,128)S(1)}, f32[16,128]{1,0:T(8,128)S(1)}, u32[]{:S(2)}, u32[]{:S(2)}) collective-permute-start(f32[16,128]{1,0:T(8,128)S(1)} %get-tuple-element.62), channel_id=1, source_target_pairs={{0,8},{16,24},{8,0},{24,16},{1,9},{17,25},{9,1},{25,17},{2,10},{18... | collective-permute-start | bytes 24584 | tf_op jit(solution)/shard_map/ppermute | solution.py:447
  6.0 6.4 %all-to-all-start = ((f32[8,16,128]{2,1,0:T(8,128)}), f32[8,16,128]{2,1,0:T(8,128)S(1)}, u32[]{:S(2)}, u32[]{:S(2)}) async-start(f32[8,16,128]{2,1,0:T(8,128)} %get-tuple-element.31), calls=%async_computation | async-start | bytes 131072 | tf_op jit(solution)/shard_map/all_to_all | solution.py:444
  12.4 0.7 %inner.1 = (f32[4,35,256]{2,1,0:T(8,128)S(1)}, f32[4,35,256]{2,1,0:T(8,128)S(1)}, f32[64,256]{1,0:T(8,128)S(1)}, f32[4,256]{1,0:T(4,128)S(1)}, f32[1,256]{1,0:T(1,128)S(1)}, /*index=5*/bf16[35,256]{1,0:T(8,128)(2,1)S(1)}) custom-call(s32[4,256]{1,0:T(4,128)S(1)} %get-tuple-element.36.code_ref, f32[280,128]{1,0:T(8,128)S(1)} %get-tuple-element.37.fields_ref, ...), custom_call_target="tpu_custom_call" | custom-call | tf_op jit(solution)/shard_map/inner/pallas_call | solution.py:451
  13.1 0.0 collective-permute-done.1
  13.1 0.0 collective-permute-done
  13.1 3.8 %all-to-all-done.refs_0_ = f32[8,16,128]{2,1,0:T(8,128)S(1)} async-done(((f32[8,16,128]{2,1,0:T(8,128)}), f32[8,16,128]{2,1,0:T(8,128)S(1)}, u32[]{:S(2)}, u32[]{:S(2)}) %all-to-all-start) | async-done | bytes 65568 | tf_op jit(solution)/shard_map/all_to_all | solution.py:444
  17.0 0.6 %outer.1 = (f32[280,128]{1,0:T(8,128)S(1)}, f32[280,128]{1,0:T(8,128)S(1)}, f32[32,1,128]{2,1,0:T(1,128)S(1)}) custom-call(f32[8,16,128]{2,1,0:T(8,128)S(1)} %all-to-all-done.refs_0_, f32[16,128]{1,0:T(8,128)S(1)} %get-tuple-element.60.refs_1_, f32[16,128]{1,0:T(8,128)S(1)} %get-tuple-element.59.refs_2_, bf16[320,1024]{1,0:T(8,128)(2,1)S(1)} %get-tuple-element.34.refs_3_, ...), custom_call_target="tpu_custom_call" | custom-call | tf_op jit(solution)/shard_map/outer/pallas_call | solution.py:464
  17.6 9.3 %all_to_all.10.refs_0_ = f32[32,1,128]{2,1,0:T(1,128)S(1)} all-to-all(f32[32,1,128]{2,1,0:T(1,128)S(1)} %get-tuple-element.53), channel_id=1, replica_groups=mesh['grp'=4,'sub'=8] {'grp','sub'}, dimensions={0} | all-to-all | bytes 32768 | tf_op jit(solution)/shard_map/all_to_all | solution.py:488
  26.9 0.7 %finish.1 = (f32[1]{0:T(128)}, f32[280,128]{1,0:T(8,128)}, f32[280,128]{1,0:T(8,128)}) custom-call(f32[32,1,128]{2,1,0:T(1,128)S(1)} %all_to_all.10.refs_0_, f32[280,128]{1,0:T(8,128)S(1)} %get-tuple-element.54.refs_1_, f32[280,128]{1,0:T(8,128)S(1)} %get-tuple-element.55.refs_2_), custom_call_target="tpu_custom_call" | custom-call | tf_op jit(solution)/shard_map/finish/pallas_call | solution.py:490
  (2 shorter events, 0.0 us)
Async XLA Ops:
  2.9 10.2 %collective-permute-start.1 = (f32[16,128]{1,0:T(8,128)S(1)}, f32[16,128]{1,0:T(8,128)S(1)}, u32[]{:S(2)}, u32[]{:S(2)}) collective-permute-start(f32[16,128]{1,0:T(8,128)S(1)} %get-tuple-element.61), channel_id=1, source_target_pairs={{8,16},{24,0},{16,8},{0,24},{9,17},{25,1},{17,9},{1,25},{10,18},{2... | collective-permute-start | bytes 24584 | tf_op jit(solution)/shard_map/ppermute | solution.py:448
  5.4 7.7 %collective-permute-start = (f32[16,128]{1,0:T(8,128)S(1)}, f32[16,128]{1,0:T(8,128)S(1)}, u32[]{:S(2)}, u32[]{:S(2)}) collective-permute-start(f32[16,128]{1,0:T(8,128)S(1)} %get-tuple-element.62), channel_id=1, source_target_pairs={{0,8},{16,24},{8,0},{24,16},{1,9},{17,25},{9,1},{25,17},{2,10},{18... | collective-permute-start | bytes 24584 | tf_op jit(solution)/shard_map/ppermute | solution.py:447
  6.0 10.9 %all-to-all-start = ((f32[8,16,128]{2,1,0:T(8,128)}), f32[8,16,128]{2,1,0:T(8,128)S(1)}, u32[]{:S(2)}, u32[]{:S(2)}) async-start(f32[8,16,128]{2,1,0:T(8,128)} %get-tuple-element.31), calls=%async_computation | async-start | bytes 131072 | tf_op jit(solution)/shard_map/all_to_all | solution.py:444
